TPU v7x, 768 devices: a whole 4x8x12 slice. The times are simulated.
768 devices in a mesh: enc: 24 (over z, core), rep: 32 (over y, x).
Axes of the slice: x: 4, y: 8, z: 12, core: 2. Of those that a mesh axis runs over, the one named last changes fastest.
Arguments:
- encoder_out: bfloat16 [3072, 32, 3200], P(('enc', 'rep')), may hold values from -600 to 600
- destination: int32 [24576, 1], P(('enc', 'rep')), may hold values from 0 to 23; in each aligned block of 32 rows (0 to 31, 32 to 63, ...) at most 2 rows name the same one
- norm_gain: float32 [12800], replicated, may hold values from 0.1 to 1.9
- norm_bias: float32 [12800], replicated, may hold values from -3 to 3
- cotangent: bfloat16 [36864, 12800], P(('enc', 'rep')), may hold values from -6 to 6
Outputs:
- visual_tokens: bfloat16 [36864, 12800], P(('enc', 'rep'))
- encoder_grad: bfloat16 [3072, 32, 3200], P(('enc', 'rep'))
- gain_grad: float32 [12800], replicated
- bias_grad: float32 [12800], replicated
Inputs may be any that keep to these rules, and one draw needn't show every extreme that they name: `destination`: in the rows of one device no owner is named by more than 2 rows, a bound that some block reaches.
All inputs are finite; a program needn't handle non-finite values.
Results may differ from a plain program's by a relative error of at most 0.001.
Values may be sent and summed in bfloat16 or wider, within the bound.
No kernel may reach another device: no remote copies, remote signals or barrier semaphores. Data moves between devices by JAX's collectives and lax.ppermute only.
A program may use at most 32 MiB of HBM per device.

v0:
```python
import math

import jax
import jax.numpy as jnp
from jax import lax
from jax.sharding import PartitionSpec as P

epsilon = 1e-05


def copy_for_each(shard, axis):
    copies = jnp.broadcast_to(shard, (lax.axis_size(axis), *shard.shape))
    return lax.all_to_all(copies, axis, split_axis=0, concat_axis=0, tiled=True)


def of_everyone(shard, axis):
    everything = copy_for_each(shard, axis)
    return jnp.sum(everything, axis=0)


def together(arrays, axis):
    flat, at, outs = (jnp.concatenate([a.reshape(-1) for a in arrays]), 0, [])
    subtotal = of_everyone(flat, axis)
    for a in arrays:
        outs.append(subtotal[at : at + a.size].reshape(a.shape))
        at += a.size
    return tuple(outs)


def shuffle_tokens(patches):
    height, across, channels = patches.shape
    grouped = patches.reshape(height // 2, 2, across // 2, 2, channels).transpose(0, 2, 1, 3, 4)
    return grouped.reshape(height // 2 * (across // 2), 4 * channels)


def unshuffle_tokens(tokens, height, across, channels):
    grouped = tokens.reshape(height // 2, across // 2, 2, 2, channels).transpose(0, 2, 1, 3, 4)
    return grouped.reshape(height, across, channels)


def norm_forward(values, norm_gain, norm_bias):
    values = values.astype(jnp.float32)
    center = jnp.mean(values, axis=-1, keepdims=True)
    spread = jnp.mean(jnp.square(values - center), axis=-1, keepdims=True)
    inverse = lax.rsqrt(spread + epsilon)
    normed = (values - center) * inverse
    return (normed, inverse, normed * norm_gain + norm_bias)


def norm_backward(upstream, normed, inverse, norm_gain):
    scaled = upstream * norm_gain
    mean_grad = jnp.mean(scaled, axis=-1, keepdims=True)
    mean_proj = jnp.mean(scaled * normed, axis=-1, keepdims=True)
    return inverse * (scaled - mean_grad - normed * mean_proj)


def body(encoder_out, destination, norm_gain, norm_bias, cotangent):
    height, across, channels = encoder_out.shape
    groups = lax.axis_size("enc")
    devices = groups * lax.axis_size("rep")
    tokens = shuffle_tokens(encoder_out)
    token_count = tokens.shape[0]
    feature_width = tokens.shape[1]
    capacity = cotangent.shape[0] // groups
    owners = destination[:, 0]
    onehot = (owners[:, None] == jnp.arange(groups, dtype=jnp.int32)[None, :]).astype(jnp.int32)
    before = jnp.cumsum(onehot, axis=0) - onehot
    places = owners * capacity + jnp.sum(before * onehot, axis=1)
    placer = (jnp.arange(groups * capacity, dtype=jnp.int32)[:, None] == places[None, :]).astype(
        jnp.bfloat16
    )
    normed, inverse, output = norm_forward(tokens, norm_gain, norm_bias)
    outgoing = jnp.dot(
        placer, output.astype(jnp.bfloat16), preferred_element_type=jnp.float32
    ).astype(jnp.bfloat16)
    arrived = lax.all_to_all(
        outgoing.reshape(groups, capacity, feature_width),
        "enc",
        split_axis=0,
        concat_axis=0,
        tiled=True,
    )
    visual = arrived.reshape(groups * capacity, feature_width)
    returned = lax.all_to_all(
        cotangent.reshape(groups, capacity, feature_width),
        "enc",
        split_axis=0,
        concat_axis=0,
        tiled=True,
    )
    upstream = jnp.dot(
        placer.T,
        returned.reshape(groups * capacity, feature_width),
        preferred_element_type=jnp.float32,
    )
    token_grad = norm_backward(upstream, normed, inverse, norm_gain).astype(jnp.bfloat16)
    gain_part = jnp.sum(upstream * normed, axis=0)
    bias_part = jnp.sum(upstream, axis=0)
    gain_total, bias_total = together((gain_part, bias_part), "rep")
    gain_total, bias_total = together((gain_total, bias_total), "enc")
    factor = 1.0 / math.sqrt(token_count * devices)
    encoder_grad = unshuffle_tokens(token_grad, height, across, channels)
    return (visual, encoder_grad, gain_total * factor, bias_total * factor)


def solution(mesh):
    placed = (
        P(("enc", "rep"), None, None),
        P(("enc", "rep"), None),
        P(),
        P(),
        P(("enc", "rep"), None),
    )
    return jax.shard_map(
        body,
        mesh=mesh,
        in_specs=placed,
        out_specs=(P(("enc", "rep"), None), P(("enc", "rep"), None, None), P(), P()),
        check_vma=False,
    )
```

profile of v0, /device:TPU:6, one launch (start us, length us, event | category | flops | bytes accessed | tf_op | source)
XLA Modules:
  0.0 309.2 jit_solution(7175327305683454127)
XLA Ops:
  0.6 2.4 reshape.94
  3.0 0.0 copy-start
  3.0 15.6 %all-to-all-start.1 = ((bf16[24,2,12800]{2,1,0:T(2,128)(2,1)}), bf16[24,2,12800]{2,1,0:T(2,128)(2,1)}, u32[]{:S(2)}, u32[]{:S(2)}) async-start(bf16[24,2,12800]{2,1,0:T(2,128)(2,1)} %reshape.94), calls=%async_computation.1 | async-start | bytes 2457600 | tf_op jit(solution)/shard_map/all_to_all | solution.py:84
  18.6 0.0 copy-done
  18.6 0.8 reshape.100
  19.4 1.3 copy.26
  20.7 0.4 fusion.8
  21.2 0.1 div.15
  21.3 2.7 reshape.98
  23.9 0.0 copy-start.3
  23.9 1.0 multiply_reduce_fusion.2
  25.0 0.0 copy-start.1
  25.0 0.1 rsqrt.12
  25.1 0.0 copy-done.3
  25.1 0.1 fusion.5
  25.2 0.1 reduce_window_sum.11
  25.2 0.2 select_reduce_fusion
  25.4 40.1 %all-to-all-done.1 = bf16[24,2,12800]{2,1,0:T(2,128)(2,1)} async-done(((bf16[24,2,12800]{2,1,0:T(2,128)(2,1)}), bf16[24,2,12800]{2,1,0:T(2,128)(2,1)}, u32[]{:S(2)}, u32[]{:S(2)}) %all-to-all-start.1) | async-done | bytes 1228832 | tf_op jit(solution)/shard_map/all_to_all | solution.py:84
  65.5 2.4 reshape.95
  67.9 0.0 copy-done.1
  67.9 2.3 multiply_reduce_fusion
  70.2 3.4 %broadcast_in_dim.4 = f32[32,1,25600]{2,1,0:T(1,128)} broadcast(f32[25600]{0:T(1024)S(1)} %pad_maximum_fusion), dimensions={2} | broadcast | bytes 3379200 | tf_op jit(solution)/shard_map/broadcast_in_dim | solution.py:12
  73.6 0.0 copy-start.2
  73.6 10.4 %all-to-all-start.2 = ((f32[32,1,25600]{2,1,0:T(1,128)}), f32[32,1,25600]{2,1,0:T(1,128)}, u32[]{:S(2)}, u32[]{:S(2)}) async-start(f32[32,1,25600]{2,1,0:T(1,128)} %broadcast_in_dim.4), calls=%async_computation.2 | async-start | bytes 6553600 | tf_op jit(solution)/shard_map/all_to_all | solution.py:13
  83.9 0.0 copy-done.2
  84.0 1.6 convolution_convert_fusion
  85.5 2.4 reshape.92
  87.9 68.7 %all-to-all-done.2 = f32[32,1,25600]{2,1,0:T(1,128)} async-done(((f32[32,1,25600]{2,1,0:T(1,128)}), f32[32,1,25600]{2,1,0:T(1,128)}, u32[]{:S(2)}, u32[]{:S(2)}) %all-to-all-start.2) | async-done | bytes 3276832 | tf_op jit(solution)/shard_map/all_to_all | solution.py:13
  156.6 8.4 %all-to-all-start = ((bf16[24,2,12800]{2,1,0:T(2,128)(2,1)}), bf16[24,2,12800]{2,1,0:T(2,128)(2,1)}, u32[]{:S(2)}, u32[]{:S(2)}) async-start(bf16[24,2,12800]{2,1,0:T(2,128)(2,1)} %reshape.92), calls=%async_computation | async-start | bytes 2457600 | tf_op jit(solution)/shard_map/all_to_all | solution.py:76
  165.0 3.8 %reduce_sum.88 = f32[25600]{0:T(1024)S(1)} reduce(f32[32,1,25600]{2,1,0:T(1,128)} %all-to-all-done.2, f32[]{:T(128)} %constant.16.clone.1), dimensions={0,1}, to_apply=%region_8.9 | reduce | flops 793600 | bytes 3379204 | tf_op jit(solution)/shard_map/reduce_sum | solution.py:18
  168.8 42.9 %all-to-all-done = bf16[24,2,12800]{2,1,0:T(2,128)(2,1)} async-done(((bf16[24,2,12800]{2,1,0:T(2,128)(2,1)}), bf16[24,2,12800]{2,1,0:T(2,128)(2,1)}, u32[]{:S(2)}, u32[]{:S(2)}) %all-to-all-start) | async-done | bytes 1228832 | tf_op jit(solution)/shard_map/all_to_all | solution.py:76
  211.7 2.7 broadcast_in_dim.5
  214.4 4.8 %all-to-all-start.3 = ((f32[24,1,25600]{2,1,0:T(1,128)}), f32[24,1,25600]{2,1,0:T(1,128)}, u32[]{:S(2)}, u32[]{:S(2)}) async-start(f32[24,1,25600]{2,1,0:T(1,128)} %broadcast_in_dim.5), calls=%async_computation.3 | async-start | bytes 4915200 | tf_op jit(solution)/shard_map/all_to_all | solution.py:13
  219.2 1.4 multiply_convert_fusion
  220.5 2.3 reshape.96
  222.9 0.6 copy.14
  223.4 1.2 reshape.97
  224.6 2.4 reshape.93
  227.0 78.4 %all-to-all-done.3 = f32[24,1,25600]{2,1,0:T(1,128)} async-done(((f32[24,1,25600]{2,1,0:T(1,128)}), f32[24,1,25600]{2,1,0:T(1,128)}, u32[]{:S(2)}, u32[]{:S(2)}) %all-to-all-start.3) | async-done | bytes 2457632 | tf_op jit(solution)/shard_map/all_to_all | solution.py:13
  305.4 3.1 %reduce_sum.89 = f32[25600]{0:T(1024)S(1)} reduce(f32[24,1,25600]{2,1,0:T(1,128)} %all-to-all-done.3, f32[]{:T(128)} %constant.16.clone.1), dimensions={0,1}, to_apply=%region_9.10 | reduce | flops 588800 | bytes 2560004 | tf_op jit(solution)/shard_map/reduce_sum | solution.py:18
  308.5 0.7 slice_multiply_fusion
  (5 shorter events, 0.0 us)
Async XLA Ops:
  3.0 15.6 %copy-start = (bf16[4,32,3200]{2,1,0:T(8,128)(2,1)S(1)}, bf16[4,32,3200]{2,1,0:T(8,128)(2,1)}, u32[]{:S(2)}) copy-start(bf16[4,32,3200]{2,1,0:T(8,128)(2,1)} %param.5) | copy-start | bytes 2457604
  3.0 62.5 %all-to-all-start.1 = ((bf16[24,2,12800]{2,1,0:T(2,128)(2,1)}), bf16[24,2,12800]{2,1,0:T(2,128)(2,1)}, u32[]{:S(2)}, u32[]{:S(2)}) async-start(bf16[24,2,12800]{2,1,0:T(2,128)(2,1)} %reshape.94), calls=%async_computation.1 | async-start | bytes 2457600 | tf_op jit(solution)/shard_map/all_to_all | solution.py:84
  23.9 1.2 copy-start.3
  25.0 42.9 %copy-start.1 = (f32[12800]{0:T(1024)S(1)}, f32[12800]{0:T(1024)}, u32[]{:S(2)}) copy-start(f32[12800]{0:T(1024)} %param.7) | copy-start | bytes 153604
  73.6 10.4 %copy-start.2 = (f32[12800]{0:T(1024)S(1)}, f32[12800]{0:T(1024)}, u32[]{:S(2)}) copy-start(f32[12800]{0:T(1024)} %param.8) | copy-start | bytes 153604
  73.6 83.0 %all-to-all-start.2 = ((f32[32,1,25600]{2,1,0:T(1,128)}), f32[32,1,25600]{2,1,0:T(1,128)}, u32[]{:S(2)}, u32[]{:S(2)}) async-start(f32[32,1,25600]{2,1,0:T(1,128)} %broadcast_in_dim.4), calls=%async_computation.2 | async-start | bytes 6553600 | tf_op jit(solution)/shard_map/all_to_all | solution.py:13
  156.6 55.1 %all-to-all-start = ((bf16[24,2,12800]{2,1,0:T(2,128)(2,1)}), bf16[24,2,12800]{2,1,0:T(2,128)(2,1)}, u32[]{:S(2)}, u32[]{:S(2)}) async-start(bf16[24,2,12800]{2,1,0:T(2,128)(2,1)} %reshape.92), calls=%async_computation | async-start | bytes 2457600 | tf_op jit(solution)/shard_map/all_to_all | solution.py:76
  214.4 91.0 %all-to-all-start.3 = ((f32[24,1,25600]{2,1,0:T(1,128)}), f32[24,1,25600]{2,1,0:T(1,128)}, u32[]{:S(2)}, u32[]{:S(2)}) async-start(f32[24,1,25600]{2,1,0:T(1,128)} %broadcast_in_dim.5), calls=%async_computation.3 | async-start | bytes 4915200 | tf_op jit(solution)/shard_map/all_to_all | solution.py:13
where the time goes:
time: 310 us; the launch traced here: 309 us
  waiting for transfers between devices  230 us (74%)
  starting transfers between devices  39.1 us (13%)
  local copies, waits for them, and re-layouts  24.6 us (8%)
  other arithmetic  10.8 us (3%)
  matrix products  3.82 us (1%)
    all_to_all x2, waiting for transfers between devices, copy_for_each(): return lax.all_to_all(copies, axis, split_axis=0, concat_axis=0, tiled=True)  147 us
    all_to_all x1, waiting for transfers between devices, body(): lax.all_to_all(outgoing.reshape(groups, capacity, feature_width), 'enc',...  42.9 us
    all_to_all x1, waiting for transfers between devices, body(): lax.all_to_all(cotangent.reshape(groups, capacity, feature_width), 'enc',...  40.1 us
    all_to_all x1, starting transfers between devices, body(): lax.all_to_all(cotangent.reshape(groups, capacity, feature_width), 'enc',...  15.6 us
    all_to_all x2, starting transfers between devices, copy_for_each(): return lax.all_to_all(copies, axis, split_axis=0, concat_axis=0, tiled=True)  15.1 us
    all_to_all x1, starting transfers between devices, body(): lax.all_to_all(outgoing.reshape(groups, capacity, feature_width), 'enc',...  8.36 us
    reduce_sum x2, other arithmetic, of_everyone(): return jnp.sum(everything, axis=0)  6.92 us
  transfers between devices with their start and end apart: 4, of which 4 were waited for; matrix products, arithmetic and copies ran while one was open for 7% of the time, Pallas kernels for 0%

commit v1 on v0

v1 whole, which is shorter than its diff:
```python
import math

import jax
import jax.numpy as jnp
import numpy as np
from jax import lax
from jax.sharding import Mesh
from jax.sharding import PartitionSpec as P


epsilon = 1e-05
ENC = ("z", "core")
REP = ("y", "x")
EACH = ENC + REP


def swapped(value, axis, flip):
    size = lax.axis_size(axis)
    return lax.ppermute(value, axis, [(i, i ^ flip) for i in range(size)])


def total_of(gain_part, bias_part):
    first = lax.axis_index("core") == 0
    mine = jnp.where(first, gain_part, bias_part)
    other = jnp.where(first, bias_part, gain_part)
    total = mine + swapped(other, "core", 1)
    for axis, flips in (("x", (1, 2)), ("y", (1, 2, 4)), ("z", (1, 2))):
        for flip in flips:
            total = total + swapped(total, axis, flip)
    deep = lax.axis_size("z")
    below = lax.ppermute(total, "z", [(i, (i + 4) % deep) for i in range(deep)])
    above = lax.ppermute(total, "z", [(i, (i - 4) % deep) for i in range(deep)])
    third = lax.axis_index("z") // 4
    zeroth = jnp.where(third == 0, total, jnp.where(third == 1, below, above))
    middle = jnp.where(third == 1, total, jnp.where(third == 2, below, above))
    last = jnp.where(third == 2, total, jnp.where(third == 0, below, above))
    total = zeroth + middle + last
    back = swapped(total, "core", 1)
    return jnp.where(first, total, back), jnp.where(first, back, total)


def shuffle_tokens(patches):
    height, across, channels = patches.shape
    grouped = patches.reshape(height // 2, 2, across // 2, 2, channels).transpose(0, 2, 1, 3, 4)
    return grouped.reshape(height // 2 * (across // 2), 4 * channels)


def unshuffle_tokens(tokens, height, across, channels):
    grouped = tokens.reshape(height // 2, across // 2, 2, 2, channels).transpose(0, 2, 1, 3, 4)
    return grouped.reshape(height, across, channels)


def norm_forward(values, norm_gain, norm_bias):
    values = values.astype(jnp.float32)
    center = jnp.mean(values, axis=-1, keepdims=True)
    spread = jnp.mean(jnp.square(values - center), axis=-1, keepdims=True)
    inverse = lax.rsqrt(spread + epsilon)
    normed = (values - center) * inverse
    return (normed, inverse, normed * norm_gain + norm_bias)


def norm_backward(upstream, normed, inverse, norm_gain):
    scaled = upstream * norm_gain
    mean_grad = jnp.mean(scaled, axis=-1, keepdims=True)
    mean_proj = jnp.mean(scaled * normed, axis=-1, keepdims=True)
    return inverse * (scaled - mean_grad - normed * mean_proj)


def steps(encoder_out, destination, norm_gain, norm_bias, cotangent):
    height, across, channels = encoder_out.shape
    groups = lax.axis_size(ENC)
    devices = groups * lax.axis_size(REP)
    tokens = shuffle_tokens(encoder_out)
    token_count = tokens.shape[0]
    feature_width = tokens.shape[1]
    capacity = cotangent.shape[0] // groups
    owners = destination[:, 0]
    onehot = (owners[:, None] == jnp.arange(groups, dtype=jnp.int32)[None, :]).astype(jnp.int32)
    before = jnp.cumsum(onehot, axis=0) - onehot
    places = owners * capacity + jnp.sum(before * onehot, axis=1)
    placer = (jnp.arange(groups * capacity, dtype=jnp.int32)[:, None] == places[None, :]).astype(
        jnp.bfloat16
    )
    normed, inverse, output = norm_forward(tokens, norm_gain, norm_bias)
    outgoing = jnp.dot(
        placer, output.astype(jnp.bfloat16), preferred_element_type=jnp.float32
    ).astype(jnp.bfloat16)
    outgoing = outgoing.reshape(groups, capacity, feature_width)
    arrived = lax.all_to_all(outgoing, ENC, split_axis=0, concat_axis=0, tiled=True)
    visual = arrived.reshape(groups * capacity, feature_width)
    slots = cotangent.reshape(groups, capacity, feature_width)
    returned = lax.all_to_all(slots, ENC, split_axis=0, concat_axis=0, tiled=True)
    upstream = jnp.dot(
        placer.T,
        returned.reshape(groups * capacity, feature_width),
        preferred_element_type=jnp.float32,
    )
    token_grad = norm_backward(upstream, normed, inverse, norm_gain).astype(jnp.bfloat16)
    gain_part = jnp.sum(upstream * normed, axis=0)
    bias_part = jnp.sum(upstream, axis=0)
    gain_total, bias_total = total_of(gain_part, bias_part)
    factor = 1.0 / math.sqrt(token_count * devices)
    encoder_grad = unshuffle_tokens(token_grad, height, across, channels)
    return (visual, encoder_grad, gain_total * factor, bias_total * factor)


def solution(mesh):
    placed = (P(EACH, None, None), P(EACH, None), P(), P(), P(EACH, None))
    fine = Mesh(np.asarray(mesh.devices).reshape(12, 2, 8, 4), EACH)
    return jax.shard_map(
        steps,
        mesh=fine,
        in_specs=placed,
        out_specs=(P(EACH, None), P(EACH, None, None), P(), P()),
        check_vma=False,
    )
```

time: 310 us -> 190 us (0.61)
  waiting for transfers between devices: 230 us -> 102 us
  starting transfers between devices: 39.1 us -> 61.5 us
  local copies, waits for them, and re-layouts: 24.6 us -> 16 us
  other arithmetic: 10.8 us -> 3.94 us
    all_to_all x4 -> x2, waiting for transfers between devices: 230 us -> 42.6 us  [the longest x1 42.6 us: steps(): lax.all_to_all(slots, ENC, split_axis=0, concat_axis=0, tiled=True)]
    ppermute x0 -> x11, waiting for transfers between devices: none -> 59.4 us  [the longest x1 35.5 us: total_of(): below = lax.ppermute(total, 'z', [(i, (i + 4) % deep) for i in range(deep)])]
    ppermute x0 -> x11, starting transfers between devices: none -> 41.2 us  [the longest x9 31.4 us: swapped(): return lax.ppermute(value, axis, [(i, i ^ flip) for i in range(size)])]
    all_to_all x4 -> x2, starting transfers between devices: 39.1 us -> 20.4 us  [the longest x1 15.6 us: steps(): lax.all_to_all(slots, ENC, split_axis=0, concat_axis=0, tiled=True)]
    reduce_sum x3 -> x1, other arithmetic: 7.1 us -> 0.18 us  [steps(): places = owners * capacity + jnp.sum(before * onehot, axis=1)]
    broadcast_in_dim x2 -> x0, local copies, waits for them, and re-layouts: 6.1 us -> none  [copy_for_each(): copies = jnp.broadcast_to(shard, (lax.axis_size(axis), *shard.shape))]
  transfers between devices with their start and end apart: 4 -> 13, of which waited for: 4 -> 10; matrix products, arithmetic and copies ran while one was open for 7% -> 9% of each run, Pallas kernels for 0% -> 0%
where the time goes in v1:
time: 190 us; the launch traced here: 188 us
  waiting for transfers between devices  102 us (54%)
  starting transfers between devices  61.5 us (32%)
  local copies, waits for them, and re-layouts  16 us (8%)
  other arithmetic  3.94 us (2%)
  matrix products  3.84 us (2%)
    all_to_all x1, waiting for transfers between devices, steps(): lax.all_to_all(slots, ENC, split_axis=0, concat_axis=0, tiled=True)  42.6 us
    ppermute x1, waiting for transfers between devices, total_of(): below = lax.ppermute(total, 'z', [(i, (i + 4) % deep) for i in range(deep)])  35.5 us
    ppermute x9, starting transfers between devices, swapped(): return lax.ppermute(value, axis, [(i, i ^ flip) for i in range(size)])  31.4 us
    ppermute x9, waiting for transfers between devices, swapped(): return lax.ppermute(value, axis, [(i, i ^ flip) for i in range(size)])  20.3 us
    all_to_all x1, starting transfers between devices, steps(): lax.all_to_all(slots, ENC, split_axis=0, concat_axis=0, tiled=True)  15.6 us
    ppermute x1, starting transfers between devices, total_of(): below = lax.ppermute(total, 'z', [(i, (i + 4) % deep) for i in range(deep)])  7.6 us
    all_to_all x1, starting transfers between devices, steps(): lax.all_to_all(outgoing, ENC, split_axis=0, concat_axis=0, tiled=True)  4.79 us
  transfers between devices with their start and end apart: 13, of which 10 were waited for; matrix products, arithmetic and copies ran while one was open for 9% of the time, Pallas kernels for 0%

profile of v1, /device:TPU:6, one launch (start us, length us, event | category | flops | bytes accessed | tf_op | source)
XLA Modules:
  0.0 188.2 jit_solution(5528968938478651299)
XLA Ops:
  0.6 2.4 %reshape.86 = bf16[24,2,12800]{2,1,0:T(2,128)(2,1)} reshape(bf16[48,12800]{1,0:T(8,128)(2,1)} %param.9) | data formatting | bytes 2457600 | tf_op jit(solution)/shard_map/reshape | solution.py:91
  3.0 15.6 %all-to-all-start.1 = ((bf16[24,2,12800]{2,1,0:T(2,128)(2,1)}), bf16[24,2,12800]{2,1,0:T(2,128)(2,1)}, u32[]{:S(2)}, u32[]{:S(2)}) async-start(bf16[24,2,12800]{2,1,0:T(2,128)(2,1)} %reshape.86), calls=%async_computation.1 | async-start | bytes 2457600 | tf_op jit(solution)/shard_map/all_to_all | solution.py:92
  18.6 0.8 reshape.92
  19.4 0.1 copy.16
  19.6 0.4 fusion.8
  20.0 0.1 div.23
  20.1 1.0 multiply_reduce_fusion.2
  21.1 0.1 rsqrt.12
  21.2 1.3 reshape.90
  22.6 0.0 copy-start.1
  22.6 0.1 fusion.5
  22.7 0.1 reduce_window_sum.11
  22.7 0.2 select_reduce_fusion
  22.9 42.6 %all-to-all-done.1 = bf16[24,2,12800]{2,1,0:T(2,128)(2,1)} async-done(((bf16[24,2,12800]{2,1,0:T(2,128)(2,1)}), bf16[24,2,12800]{2,1,0:T(2,128)(2,1)}, u32[]{:S(2)}, u32[]{:S(2)}) %all-to-all-start.1) | async-done | bytes 1228832 | tf_op jit(solution)/shard_map/all_to_all | solution.py:92
  65.5 2.4 %reshape.87 = bf16[48,12800]{1,0:T(8,128)(2,1)} reshape(bf16[24,2,12800]{2,1,0:T(2,128)(2,1)} %all-to-all-done.1) | data formatting | bytes 2457600 | tf_op jit(solution)/shard_map/reshape | solution.py:95
  67.9 2.3 %multiply_reduce_fusion = (f32[12800]{0:T(1024)S(1)}, f32[32]{0:T(128)S(1)}, f32[32]{0:T(128)S(1)}, f32[12800]{0:T(1024)S(1)}, f32[32,12800]{1,0:T(8,128)S(1)}) fusion(f32[32,12800]{1,0:T(8,128)S(1)} %reshape.90, f32[32]{0:T(128)S(1)} %rsqrt.12, f32[32]{0:T(128)S(1)} %div.23, f32[12800]{0:T(1024)S(1)} %copy-done.1, bf16[48,12800]{1,0:T(8,128)(2,1)} %reshape.87, ...), kind=kOutput, calls=%fused_computation.2 | convolution fusion | flops 42983872 | bytes 4659840 | tf_op jit(solution)/shard_map/dot_general | solution.py:93
  70.2 1.9 %collective-permute-start = (f32[12800]{0:T(1024)S(1)}, f32[12800]{0:T(1024)S(1)}, u32[]{:S(2)}, u32[]{:S(2)}) collective-permute-start(f32[12800]{0:T(1024)S(1)} %broadcast_select_fusion), channel_id=1, source_target_pairs={{0,32},{32,0},{1,33},{33,1},{2,34},{34,2},{3,35},{35,3},{4,36},{36... | collective-permute-start | bytes 153608 | tf_op jit(solution)/shard_map/ppermute | solution.py:19
  72.1 1.2 collective-permute-done
  73.3 2.7 %collective-permute-start.1 = (f32[12800]{0:T(1024)S(1)}, f32[12800]{0:T(1024)S(1)}, u32[]{:S(2)}, u32[]{:S(2)}) collective-permute-start(f32[12800]{0:T(1024)S(1)} %select_add_fusion.1), channel_id=1, source_target_pairs={{0,1},{1,0},{2,3},{3,2},{4,5},{5,4},{6,7},{7,6},{8,9},{9,8},{10,11... | collective-permute-start | bytes 153608 | tf_op jit(solution)/shard_map/ppermute | solution.py:19
  76.1 3.3 %collective-permute-done.1 = f32[12800]{0:T(1024)S(1)} collective-permute-done((f32[12800]{0:T(1024)S(1)}, f32[12800]{0:T(1024)S(1)}, u32[]{:S(2)}, u32[]{:S(2)}) %collective-permute-start.1) | collective-permute-done | bytes 51232 | tf_op jit(solution)/shard_map/ppermute | solution.py:19
  79.3 3.3 %collective-permute-start.2 = (f32[12800]{0:T(1024)S(1)}, f32[12800]{0:T(1024)S(1)}, u32[]{:S(2)}, u32[]{:S(2)}) collective-permute-start(f32[12800]{0:T(1024)S(1)} %add.64), channel_id=1, source_target_pairs={{0,2},{1,3},{2,0},{3,1},{4,6},{5,7},{6,4},{7,5},{8,10},{9,11},{10,... | collective-permute-start | bytes 153608 | tf_op jit(solution)/shard_map/ppermute | solution.py:19
  82.7 4.2 %collective-permute-done.2 = f32[12800]{0:T(1024)S(1)} collective-permute-done((f32[12800]{0:T(1024)S(1)}, f32[12800]{0:T(1024)S(1)}, u32[]{:S(2)}, u32[]{:S(2)}) %collective-permute-start.2) | collective-permute-done | bytes 51232 | tf_op jit(solution)/shard_map/ppermute | solution.py:19
  86.9 3.5 %collective-permute-start.3 = (f32[12800]{0:T(1024)S(1)}, f32[12800]{0:T(1024)S(1)}, u32[]{:S(2)}, u32[]{:S(2)}) collective-permute-start(f32[12800]{0:T(1024)S(1)} %add.65), channel_id=1, source_target_pairs={{0,4},{4,0},{8,12},{12,8},{16,20},{20,16},{24,28},{28,24},{1,5},{5... | collective-permute-start | bytes 153608 | tf_op jit(solution)/shard_map/ppermute | solution.py:19
  90.4 2.5 %collective-permute-done.3 = f32[12800]{0:T(1024)S(1)} collective-permute-done((f32[12800]{0:T(1024)S(1)}, f32[12800]{0:T(1024)S(1)}, u32[]{:S(2)}, u32[]{:S(2)}) %collective-permute-start.3) | collective-permute-done | bytes 51232 | tf_op jit(solution)/shard_map/ppermute | solution.py:19
  92.9 4.5 %collective-permute-start.4 = (f32[12800]{0:T(1024)S(1)}, f32[12800]{0:T(1024)S(1)}, u32[]{:S(2)}, u32[]{:S(2)}) collective-permute-start(f32[12800]{0:T(1024)S(1)} %add.66), channel_id=1, source_target_pairs={{0,8},{4,12},{8,0},{12,4},{16,24},{20,28},{24,16},{28,20},{1,9},{5... | collective-permute-start | bytes 153608 | tf_op jit(solution)/shard_map/ppermute | solution.py:19
  97.4 2.4 %collective-permute-done.4 = f32[12800]{0:T(1024)S(1)} collective-permute-done((f32[12800]{0:T(1024)S(1)}, f32[12800]{0:T(1024)S(1)}, u32[]{:S(2)}, u32[]{:S(2)}) %collective-permute-start.4) | collective-permute-done | bytes 51232 | tf_op jit(solution)/shard_map/ppermute | solution.py:19
  99.9 8.4 %collective-permute-start.5 = (f32[12800]{0:T(1024)S(1)}, f32[12800]{0:T(1024)S(1)}, u32[]{:S(2)}, u32[]{:S(2)}) collective-permute-start(f32[12800]{0:T(1024)S(1)} %add.67), channel_id=1, source_target_pairs={{0,16},{4,20},{8,24},{12,28},{16,0},{20,4},{24,8},{28,12},{1,17},{... | collective-permute-start | bytes 153608 | tf_op jit(solution)/shard_map/ppermute | solution.py:19
  108.3 2.2 %collective-permute-done.5 = f32[12800]{0:T(1024)S(1)} collective-permute-done((f32[12800]{0:T(1024)S(1)}, f32[12800]{0:T(1024)S(1)}, u32[]{:S(2)}, u32[]{:S(2)}) %collective-permute-start.5) | collective-permute-done | bytes 51232 | tf_op jit(solution)/shard_map/ppermute | solution.py:19
  110.5 1.9 %collective-permute-start.6 = (f32[12800]{0:T(1024)S(1)}, f32[12800]{0:T(1024)S(1)}, u32[]{:S(2)}, u32[]{:S(2)}) collective-permute-start(f32[12800]{0:T(1024)S(1)} %add.68), channel_id=1, source_target_pairs={{0,64},{64,0},{128,192},{192,128},{256,320},{320,256},{384,448},{4... | collective-permute-start | bytes 153608 | tf_op jit(solution)/shard_map/ppermute | solution.py:19
  112.4 4.4 %collective-permute-done.6 = f32[12800]{0:T(1024)S(1)} collective-permute-done((f32[12800]{0:T(1024)S(1)}, f32[12800]{0:T(1024)S(1)}, u32[]{:S(2)}, u32[]{:S(2)}) %collective-permute-start.6) | collective-permute-done | bytes 51232 | tf_op jit(solution)/shard_map/ppermute | solution.py:19
  116.8 3.2 %collective-permute-start.7 = (f32[12800]{0:T(1024)S(1)}, f32[12800]{0:T(1024)S(1)}, u32[]{:S(2)}, u32[]{:S(2)}) collective-permute-start(f32[12800]{0:T(1024)S(1)} %add.69), channel_id=1, source_target_pairs={{0,128},{64,192},{128,0},{192,64},{256,384},{320,448},{384,256},{4... | collective-permute-start | bytes 153608 | tf_op jit(solution)/shard_map/ppermute | solution.py:19
  120.1 1.6 convolution_convert_fusion
  121.6 2.4 %reshape.84 = bf16[24,2,12800]{2,1,0:T(2,128)(2,1)} reshape(bf16[48,12800]{1,0:T(8,128)(2,1)} %convolution_convert_fusion) | data formatting | bytes 2457600 | tf_op jit(solution)/shard_map/reshape | solution.py:88
  124.0 4.8 %all-to-all-start = ((bf16[24,2,12800]{2,1,0:T(2,128)(2,1)}), bf16[24,2,12800]{2,1,0:T(2,128)(2,1)}, u32[]{:S(2)}, u32[]{:S(2)}) async-start(bf16[24,2,12800]{2,1,0:T(2,128)(2,1)} %reshape.84), calls=%async_computation | async-start | bytes 2457600 | tf_op jit(solution)/shard_map/all_to_all | solution.py:89
  128.8 0.0 collective-permute-done.7
  128.9 7.6 %collective-permute-start.8 = (f32[12800]{0:T(1024)S(1)}, f32[12800]{0:T(1024)S(1)}, u32[]{:S(2)}, u32[]{:S(2)}) collective-permute-start(f32[12800]{0:T(1024)S(1)} %add.70), channel_id=1, source_target_pairs={{0,256},{64,320},{128,384},{192,448},{256,512},{320,576},{384,640}... | collective-permute-start | bytes 153608 | tf_op jit(solution)/shard_map/ppermute | solution.py:31
  136.5 2.2 %collective-permute-start.9 = (f32[12800]{0:T(1024)S(1)}, f32[12800]{0:T(1024)S(1)}, u32[]{:S(2)}, u32[]{:S(2)}) collective-permute-start(f32[12800]{0:T(1024)S(1)} %add.70), channel_id=1, source_target_pairs={{0,512},{64,576},{128,640},{192,704},{256,0},{320,64},{384,128},{4... | collective-permute-start | bytes 153608 | tf_op jit(solution)/shard_map/ppermute | solution.py:32
  138.7 35.5 %collective-permute-done.8 = f32[12800]{0:T(1024)S(1)} collective-permute-done((f32[12800]{0:T(1024)S(1)}, f32[12800]{0:T(1024)S(1)}, u32[]{:S(2)}, u32[]{:S(2)}) %collective-permute-start.8) | collective-permute-done | bytes 51232 | tf_op jit(solution)/shard_map/ppermute | solution.py:31
  174.1 3.7 %collective-permute-done.9 = f32[12800]{0:T(1024)S(1)} collective-permute-done((f32[12800]{0:T(1024)S(1)}, f32[12800]{0:T(1024)S(1)}, u32[]{:S(2)}, u32[]{:S(2)}) %collective-permute-start.9) | collective-permute-done | bytes 51232 | tf_op jit(solution)/shard_map/ppermute | solution.py:32
  177.8 1.9 %collective-permute-start.10 = (f32[12800]{0:T(1024)S(1)}, f32[12800]{0:T(1024)S(1)}, u32[]{:S(2)}, u32[]{:S(2)}) collective-permute-start(f32[12800]{0:T(1024)S(1)} %select_add_fusion), channel_id=1, source_target_pairs={{0,32},{32,0},{1,33},{33,1},{2,34},{34,2},{3,35},{35,3},{4,36},{36... | collective-permute-start | bytes 153608 | tf_op jit(solution)/shard_map/ppermute | solution.py:19
  179.8 1.4 multiply_convert_fusion
  181.1 2.3 %reshape.88 = bf16[2,16,2,2,3200]{4,3,2,1,0:T(2,128)(2,1)S(1)} reshape(bf16[32,12800]{1,0:T(8,128)(2,1)} %multiply_convert_fusion) | data formatting | bytes 1638400 | tf_op jit(solution)/shard_map/reshape | solution.py:49
  183.4 0.6 copy.10
  184.0 1.2 reshape.89
  185.2 0.0 all-to-all-done
  185.2 2.4 %reshape.85 = bf16[48,12800]{1,0:T(8,128)(2,1)} reshape(bf16[24,2,12800]{2,1,0:T(2,128)(2,1)} %all-to-all-done) | data formatting | bytes 2457600 | tf_op jit(solution)/shard_map/reshape | solution.py:90
  187.6 0.0 collective-permute-done.10
  187.6 0.7 select_multiply_fusion
  (21 shorter events, 0.1 us)
Async XLA Ops:
  3.0 15.6 %copy-start = (bf16[4,32,3200]{2,1,0:T(8,128)(2,1)S(1)}, bf16[4,32,3200]{2,1,0:T(8,128)(2,1)}, u32[]{:S(2)}) copy-start(bf16[4,32,3200]{2,1,0:T(8,128)(2,1)} %param.5) | copy-start | bytes 2457604
  3.0 62.5 %all-to-all-start.1 = ((bf16[24,2,12800]{2,1,0:T(2,128)(2,1)}), bf16[24,2,12800]{2,1,0:T(2,128)(2,1)}, u32[]{:S(2)}, u32[]{:S(2)}) async-start(bf16[24,2,12800]{2,1,0:T(2,128)(2,1)} %reshape.86), calls=%async_computation.1 | async-start | bytes 2457600 | tf_op jit(solution)/shard_map/all_to_all | solution.py:92
  21.2 1.3 copy-start.3
  22.6 45.3 %copy-start.1 = (f32[12800]{0:T(1024)S(1)}, f32[12800]{0:T(1024)}, u32[]{:S(2)}) copy-start(f32[12800]{0:T(1024)} %param.7) | copy-start | bytes 153604
  67.9 52.2 %copy-start.2 = (f32[12800]{0:T(1024)S(1)}, f32[12800]{0:T(1024)}, u32[]{:S(2)}) copy-start(f32[12800]{0:T(1024)} %param.8) | copy-start | bytes 153604
  70.2 3.1 %collective-permute-start = (f32[12800]{0:T(1024)S(1)}, f32[12800]{0:T(1024)S(1)}, u32[]{:S(2)}, u32[]{:S(2)}) collective-permute-start(f32[12800]{0:T(1024)S(1)} %broadcast_select_fusion), channel_id=1, source_target_pairs={{0,32},{32,0},{1,33},{33,1},{2,34},{34,2},{3,35},{35,3},{4,36},{36... | collective-permute-start | bytes 153608 | tf_op jit(solution)/shard_map/ppermute | solution.py:19
  73.3 6.0 %collective-permute-start.1 = (f32[12800]{0:T(1024)S(1)}, f32[12800]{0:T(1024)S(1)}, u32[]{:S(2)}, u32[]{:S(2)}) collective-permute-start(f32[12800]{0:T(1024)S(1)} %select_add_fusion.1), channel_id=1, source_target_pairs={{0,1},{1,0},{2,3},{3,2},{4,5},{5,4},{6,7},{7,6},{8,9},{9,8},{10,11... | collective-permute-start | bytes 153608 | tf_op jit(solution)/shard_map/ppermute | solution.py:19
  79.3 7.5 %collective-permute-start.2 = (f32[12800]{0:T(1024)S(1)}, f32[12800]{0:T(1024)S(1)}, u32[]{:S(2)}, u32[]{:S(2)}) collective-permute-start(f32[12800]{0:T(1024)S(1)} %add.64), channel_id=1, source_target_pairs={{0,2},{1,3},{2,0},{3,1},{4,6},{5,7},{6,4},{7,5},{8,10},{9,11},{10,... | collective-permute-start | bytes 153608 | tf_op jit(solution)/shard_map/ppermute | solution.py:19
  86.9 6.0 %collective-permute-start.3 = (f32[12800]{0:T(1024)S(1)}, f32[12800]{0:T(1024)S(1)}, u32[]{:S(2)}, u32[]{:S(2)}) collective-permute-start(f32[12800]{0:T(1024)S(1)} %add.65), channel_id=1, source_target_pairs={{0,4},{4,0},{8,12},{12,8},{16,20},{20,16},{24,28},{28,24},{1,5},{5... | collective-permute-start | bytes 153608 | tf_op jit(solution)/shard_map/ppermute | solution.py:19
  92.9 6.9 %collective-permute-start.4 = (f32[12800]{0:T(1024)S(1)}, f32[12800]{0:T(1024)S(1)}, u32[]{:S(2)}, u32[]{:S(2)}) collective-permute-start(f32[12800]{0:T(1024)S(1)} %add.66), channel_id=1, source_target_pairs={{0,8},{4,12},{8,0},{12,4},{16,24},{20,28},{24,16},{28,20},{1,9},{5... | collective-permute-start | bytes 153608 | tf_op jit(solution)/shard_map/ppermute | solution.py:19
  99.9 10.6 %collective-permute-start.5 = (f32[12800]{0:T(1024)S(1)}, f32[12800]{0:T(1024)S(1)}, u32[]{:S(2)}, u32[]{:S(2)}) collective-permute-start(f32[12800]{0:T(1024)S(1)} %add.67), channel_id=1, source_target_pairs={{0,16},{4,20},{8,24},{12,28},{16,0},{20,4},{24,8},{28,12},{1,17},{... | collective-permute-start | bytes 153608 | tf_op jit(solution)/shard_map/ppermute | solution.py:19
  110.5 6.3 %collective-permute-start.6 = (f32[12800]{0:T(1024)S(1)}, f32[12800]{0:T(1024)S(1)}, u32[]{:S(2)}, u32[]{:S(2)}) collective-permute-start(f32[12800]{0:T(1024)S(1)} %add.68), channel_id=1, source_target_pairs={{0,64},{64,0},{128,192},{192,128},{256,320},{320,256},{384,448},{4... | collective-permute-start | bytes 153608 | tf_op jit(solution)/shard_map/ppermute | solution.py:19
  116.8 12.1 %collective-permute-start.7 = (f32[12800]{0:T(1024)S(1)}, f32[12800]{0:T(1024)S(1)}, u32[]{:S(2)}, u32[]{:S(2)}) collective-permute-start(f32[12800]{0:T(1024)S(1)} %add.69), channel_id=1, source_target_pairs={{0,128},{64,192},{128,0},{192,64},{256,384},{320,448},{384,256},{4... | collective-permute-start | bytes 153608 | tf_op jit(solution)/shard_map/ppermute | solution.py:19
  124.0 61.2 %all-to-all-start = ((bf16[24,2,12800]{2,1,0:T(2,128)(2,1)}), bf16[24,2,12800]{2,1,0:T(2,128)(2,1)}, u32[]{:S(2)}, u32[]{:S(2)}) async-start(bf16[24,2,12800]{2,1,0:T(2,128)(2,1)} %reshape.84), calls=%async_computation | async-start | bytes 2457600 | tf_op jit(solution)/shard_map/all_to_all | solution.py:89
  128.9 45.3 %collective-permute-start.8 = (f32[12800]{0:T(1024)S(1)}, f32[12800]{0:T(1024)S(1)}, u32[]{:S(2)}, u32[]{:S(2)}) collective-permute-start(f32[12800]{0:T(1024)S(1)} %add.70), channel_id=1, source_target_pairs={{0,256},{64,320},{128,384},{192,448},{256,512},{320,576},{384,640}... | collective-permute-start | bytes 153608 | tf_op jit(solution)/shard_map/ppermute | solution.py:31
  136.5 41.3 %collective-permute-start.9 = (f32[12800]{0:T(1024)S(1)}, f32[12800]{0:T(1024)S(1)}, u32[]{:S(2)}, u32[]{:S(2)}) collective-permute-start(f32[12800]{0:T(1024)S(1)} %add.70), channel_id=1, source_target_pairs={{0,512},{64,576},{128,640},{192,704},{256,0},{320,64},{384,128},{4... | collective-permute-start | bytes 153608 | tf_op jit(solution)/shard_map/ppermute | solution.py:32
  177.8 9.8 %collective-permute-start.10 = (f32[12800]{0:T(1024)S(1)}, f32[12800]{0:T(1024)S(1)}, u32[]{:S(2)}, u32[]{:S(2)}) collective-permute-start(f32[12800]{0:T(1024)S(1)} %select_add_fusion), channel_id=1, source_target_pairs={{0,32},{32,0},{1,33},{33,1},{2,34},{34,2},{3,35},{35,3},{4,36},{36... | collective-permute-start | bytes 153608 | tf_op jit(solution)/shard_map/ppermute | solution.py:19

commit v2 on v1

--- a/solution.py
+++ b/solution.py
@@ -9,7 +9,7 @@
 
 
 epsilon = 1e-05
-ENC = ("z", "core")
+ENC = ("zh", "zl", "core")
 REP = ("y", "x")
 EACH = ENC + REP
 
@@ -19,22 +19,22 @@
     return lax.ppermute(value, axis, [(i, i ^ flip) for i in range(size)])
 
 
+def of_everyone(value, axis):
+    copies = jnp.broadcast_to(value, (lax.axis_size(axis), *value.shape))
+    everything = lax.all_to_all(copies, axis, split_axis=0, concat_axis=0, tiled=True)
+    return jnp.sum(everything, axis=0)
+
+
 def total_of(gain_part, bias_part):
     first = lax.axis_index("core") == 0
     mine = jnp.where(first, gain_part, bias_part)
     other = jnp.where(first, bias_part, gain_part)
     total = mine + swapped(other, "core", 1)
-    for axis, flips in (("x", (1, 2)), ("y", (1, 2, 4)), ("z", (1, 2))):
+    for axis, flips in (("x", (1, 2)), ("y", (1, 2, 4))):
         for flip in flips:
             total = total + swapped(total, axis, flip)
-    deep = lax.axis_size("z")
-    below = lax.ppermute(total, "z", [(i, (i + 4) % deep) for i in range(deep)])
-    above = lax.ppermute(total, "z", [(i, (i - 4) % deep) for i in range(deep)])
-    third = lax.axis_index("z") // 4
-    zeroth = jnp.where(third == 0, total, jnp.where(third == 1, below, above))
-    middle = jnp.where(third == 1, total, jnp.where(third == 2, below, above))
-    last = jnp.where(third == 2, total, jnp.where(third == 0, below, above))
-    total = zeroth + middle + last
+    for axis in ("zl", "zh"):
+        total = of_everyone(total, axis)
     back = swapped(total, "core", 1)
     return jnp.where(first, total, back), jnp.where(first, back, total)
 
@@ -46,8 +46,8 @@
 
 
 def unshuffle_tokens(tokens, height, across, channels):
-    grouped = tokens.reshape(height // 2, across // 2, 2, 2, channels).transpose(0, 2, 1, 3, 4)
-    return grouped.reshape(height, across, channels)
+    grouped = tokens.reshape(height // 2, across // 2, 2, 2, channels)
+    return grouped.transpose(0, 2, 1, 3, 4).reshape(height, across, channels)
 
 
 def norm_forward(values, norm_gain, norm_bias):
@@ -63,7 +63,7 @@
     scaled = upstream * norm_gain
     mean_grad = jnp.mean(scaled, axis=-1, keepdims=True)
     mean_proj = jnp.mean(scaled * normed, axis=-1, keepdims=True)
-    return inverse * (scaled - mean_grad - normed * mean_proj)
+    return (inverse * (scaled - mean_grad - normed * mean_proj)).astype(jnp.bfloat16)
 
 
 def steps(encoder_out, destination, norm_gain, norm_bias, cotangent):
@@ -95,7 +95,7 @@
         returned.reshape(groups * capacity, feature_width),
         preferred_element_type=jnp.float32,
     )
-    token_grad = norm_backward(upstream, normed, inverse, norm_gain).astype(jnp.bfloat16)
+    token_grad = norm_backward(upstream, normed, inverse, norm_gain)
     gain_part = jnp.sum(upstream * normed, axis=0)
     bias_part = jnp.sum(upstream, axis=0)
     gain_total, bias_total = total_of(gain_part, bias_part)
@@ -106,7 +106,7 @@
 
 def solution(mesh):
     placed = (P(EACH, None, None), P(EACH, None), P(), P(), P(EACH, None))
-    fine = Mesh(np.asarray(mesh.devices).reshape(12, 2, 8, 4), EACH)
+    fine = Mesh(np.asarray(mesh.devices).reshape(3, 4, 2, 8, 4), EACH)
     return jax.shard_map(
         steps,
         mesh=fine,

time: 190 us -> 193 us (1.016)
  starting transfers between devices: 61.5 us -> 51.8 us
  blocking collectives: 0 us -> 9.52 us
    ppermute x2 -> x0, waiting for transfers between devices: 39.1 us -> none  [the longest x1 35.5 us: total_of(): below = lax.ppermute(total, 'z', [(i, (i + 4) % deep) for i in range(deep)])]
    all_to_all x1, waiting for transfers between devices: 0.01 us -> 38.5 us  [steps(): lax.all_to_all(outgoing, ENC, split_axis=0, concat_axis=0, tiled=True)]
    ppermute x2 -> x0, starting transfers between devices: 9.75 us -> none  [the longest x1 7.6 us: total_of(): below = lax.ppermute(total, 'z', [(i, (i + 4) % deep) for i in range(deep)])]
    all_to_all x0 -> x1, blocking collectives: none -> 9.52 us  [of_everyone(): lax.all_to_all(copies, axis, split_axis=0, concat_axis=0, tiled=True)]
    all_to_all x0 -> x1, starting transfers between devices: none -> 5.2 us  [of_everyone(): lax.all_to_all(copies, axis, split_axis=0, concat_axis=0, tiled=True)]
    all_to_all x0 -> x1, waiting for transfers between devices: none -> 5.1 us  [of_everyone(): lax.all_to_all(copies, axis, split_axis=0, concat_axis=0, tiled=True)]
    ppermute x9 -> x7, starting transfers between devices: 31.4 us -> 26.4 us  [swapped(): return lax.ppermute(value, axis, [(i, i ^ flip) for i in range(size)])]
    ppermute x9 -> x7, waiting for transfers between devices: 20.3 us -> 15.9 us  [swapped(): return lax.ppermute(value, axis, [(i, i ^ flip) for i in range(size)])]
  transfers between devices with their start and end apart: 13 -> 10, of which waited for: 10 -> 9; matrix products, arithmetic and copies ran while one was open for 9% -> 9% of each run, Pallas kernels for 0% -> 0%
where the time goes in v2:
time: 193 us; the launch traced here: 192 us
  waiting for transfers between devices  102 us (53%)
  starting transfers between devices  51.8 us (27%)
  local copies, waits for them, and re-layouts  17.7 us (9%)
  blocking collectives  9.52 us (5%)
  other arithmetic  5.56 us (3%)
  matrix products  4.63 us (2%)
    all_to_all x1, waiting for transfers between devices, steps(): lax.all_to_all(slots, ENC, split_axis=0, concat_axis=0, tiled=True)  42.6 us
    all_to_all x1, waiting for transfers between devices, steps(): lax.all_to_all(outgoing, ENC, split_axis=0, concat_axis=0, tiled=True)  38.5 us
    ppermute x7, starting transfers between devices, swapped(): return lax.ppermute(value, axis, [(i, i ^ flip) for i in range(size)])  26.4 us
    ppermute x7, waiting for transfers between devices, swapped(): return lax.ppermute(value, axis, [(i, i ^ flip) for i in range(size)])  15.9 us
    all_to_all x1, starting transfers between devices, steps(): lax.all_to_all(slots, ENC, split_axis=0, concat_axis=0, tiled=True)  15.6 us
    all_to_all x1, blocking collectives, of_everyone(): lax.all_to_all(copies, axis, split_axis=0, concat_axis=0, tiled=True)  9.52 us
    all_to_all x1, starting transfers between devices, of_everyone(): lax.all_to_all(copies, axis, split_axis=0, concat_axis=0, tiled=True)  5.2 us
    all_to_all x1, waiting for transfers between devices, of_everyone(): lax.all_to_all(copies, axis, split_axis=0, concat_axis=0, tiled=True)  5.1 us
  transfers between devices with their start and end apart: 10, of which 9 were waited for; matrix products, arithmetic and copies ran while one was open for 9% of the time, Pallas kernels for 0%

profile of v2, /device:TPU:6, one launch (start us, length us, event | category | flops | bytes accessed | tf_op | source)
XLA Modules:
  0.0 192.1 jit_solution(7959647415192494634)
XLA Ops:
  0.6 2.4 %reshape.94 = bf16[24,2,12800]{2,1,0:T(2,128)(2,1)} reshape(bf16[48,12800]{1,0:T(8,128)(2,1)} %param.9) | data formatting | bytes 2457600 | tf_op jit(solution)/shard_map/reshape | solution.py:91
  3.0 15.6 %all-to-all-start.1 = ((bf16[24,2,12800]{2,1,0:T(2,128)(2,1)}), bf16[24,2,12800]{2,1,0:T(2,128)(2,1)}, u32[]{:S(2)}, u32[]{:S(2)}) async-start(bf16[24,2,12800]{2,1,0:T(2,128)(2,1)} %reshape.94), calls=%async_computation.1 | async-start | bytes 2457600 | tf_op jit(solution)/shard_map/all_to_all | solution.py:92
  18.6 0.8 reshape.100
  19.4 0.1 copy.22
  19.6 0.4 fusion.8
  20.0 0.1 div.15
  20.1 1.0 multiply_reduce_fusion.2
  21.1 0.1 rsqrt.12
  21.2 1.3 reshape.98
  22.6 0.0 copy-start.1
  22.6 0.1 fusion.5
  22.7 0.1 reduce_window_sum.11
  22.7 0.2 select_reduce_fusion
  22.9 42.6 %all-to-all-done.1 = bf16[24,2,12800]{2,1,0:T(2,128)(2,1)} async-done(((bf16[24,2,12800]{2,1,0:T(2,128)(2,1)}), bf16[24,2,12800]{2,1,0:T(2,128)(2,1)}, u32[]{:S(2)}, u32[]{:S(2)}) %all-to-all-start.1) | async-done | bytes 1228832 | tf_op jit(solution)/shard_map/all_to_all | solution.py:92
  65.5 2.4 %reshape.95 = bf16[48,12800]{1,0:T(8,128)(2,1)} reshape(bf16[24,2,12800]{2,1,0:T(2,128)(2,1)} %all-to-all-done.1) | data formatting | bytes 2457600 | tf_op jit(solution)/shard_map/reshape | solution.py:95
  67.9 2.3 %multiply_reduce_fusion = (f32[12800]{0:T(1024)S(1)}, f32[32]{0:T(128)S(1)}, f32[32]{0:T(128)S(1)}, f32[12800]{0:T(1024)S(1)}, f32[32,12800]{1,0:T(8,128)S(1)}) fusion(f32[32,12800]{1,0:T(8,128)S(1)} %reshape.98, f32[32]{0:T(128)S(1)} %rsqrt.12, f32[32]{0:T(128)S(1)} %div.15, f32[12800]{0:T(1024)S(1)} %copy-done.1, bf16[48,12800]{1,0:T(8,128)(2,1)} %reshape.95, ...), kind=kOutput, calls=%fused_computation.2 | convolution fusion | flops 42983872 | bytes 4659840 | tf_op jit(solution)/shard_map/dot_general | solution.py:93
  70.2 1.9 collective-permute-start
  72.1 1.2 collective-permute-done
  73.3 2.7 %collective-permute-start.1 = (f32[12800]{0:T(1024)S(1)}, f32[12800]{0:T(1024)S(1)}, u32[]{:S(2)}, u32[]{:S(2)}) collective-permute-start(f32[12800]{0:T(1024)S(1)} %select_add_fusion), channel_id=1, source_target_pairs={{0,1},{1,0},{2,3},{3,2},{4,5},{5,4},{6,7},{7,6},{8,9},{9,8},{10,11... | collective-permute-start | bytes 153608 | tf_op jit(solution)/shard_map/ppermute | solution.py:19
  76.0 3.3 %collective-permute-done.1 = f32[12800]{0:T(1024)S(1)} collective-permute-done((f32[12800]{0:T(1024)S(1)}, f32[12800]{0:T(1024)S(1)}, u32[]{:S(2)}, u32[]{:S(2)}) %collective-permute-start.1) | collective-permute-done | bytes 51232 | tf_op jit(solution)/shard_map/ppermute | solution.py:19
  79.3 3.3 %collective-permute-start.2 = (f32[12800]{0:T(1024)S(1)}, f32[12800]{0:T(1024)S(1)}, u32[]{:S(2)}, u32[]{:S(2)}) collective-permute-start(f32[12800]{0:T(1024)S(1)} %add.51), channel_id=1, source_target_pairs={{0,2},{1,3},{2,0},{3,1},{4,6},{5,7},{6,4},{7,5},{8,10},{9,11},{10,... | collective-permute-start | bytes 153608 | tf_op jit(solution)/shard_map/ppermute | solution.py:19
  82.7 4.2 %collective-permute-done.2 = f32[12800]{0:T(1024)S(1)} collective-permute-done((f32[12800]{0:T(1024)S(1)}, f32[12800]{0:T(1024)S(1)}, u32[]{:S(2)}, u32[]{:S(2)}) %collective-permute-start.2) | collective-permute-done | bytes 51232 | tf_op jit(solution)/shard_map/ppermute | solution.py:19
  86.9 3.5 %collective-permute-start.3 = (f32[12800]{0:T(1024)S(1)}, f32[12800]{0:T(1024)S(1)}, u32[]{:S(2)}, u32[]{:S(2)}) collective-permute-start(f32[12800]{0:T(1024)S(1)} %add.52), channel_id=1, source_target_pairs={{0,4},{4,0},{8,12},{12,8},{16,20},{20,16},{24,28},{28,24},{1,5},{5... | collective-permute-start | bytes 153608 | tf_op jit(solution)/shard_map/ppermute | solution.py:19
  90.4 2.5 %collective-permute-done.3 = f32[12800]{0:T(1024)S(1)} collective-permute-done((f32[12800]{0:T(1024)S(1)}, f32[12800]{0:T(1024)S(1)}, u32[]{:S(2)}, u32[]{:S(2)}) %collective-permute-start.3) | collective-permute-done | bytes 51232 | tf_op jit(solution)/shard_map/ppermute | solution.py:19
  92.9 4.5 %collective-permute-start.4 = (f32[12800]{0:T(1024)S(1)}, f32[12800]{0:T(1024)S(1)}, u32[]{:S(2)}, u32[]{:S(2)}) collective-permute-start(f32[12800]{0:T(1024)S(1)} %add.53), channel_id=1, source_target_pairs={{0,8},{4,12},{8,0},{12,4},{16,24},{20,28},{24,16},{28,20},{1,9},{5... | collective-permute-start | bytes 153608 | tf_op jit(solution)/shard_map/ppermute | solution.py:19
  97.4 2.4 %collective-permute-done.4 = f32[12800]{0:T(1024)S(1)} collective-permute-done((f32[12800]{0:T(1024)S(1)}, f32[12800]{0:T(1024)S(1)}, u32[]{:S(2)}, u32[]{:S(2)}) %collective-permute-start.4) | collective-permute-done | bytes 51232 | tf_op jit(solution)/shard_map/ppermute | solution.py:19
  99.9 8.4 %collective-permute-start.5 = (f32[12800]{0:T(1024)S(1)}, f32[12800]{0:T(1024)S(1)}, u32[]{:S(2)}, u32[]{:S(2)}) collective-permute-start(f32[12800]{0:T(1024)S(1)} %add.54), channel_id=1, source_target_pairs={{0,16},{4,20},{8,24},{12,28},{16,0},{20,4},{24,8},{28,12},{1,17},{... | collective-permute-start | bytes 153608 | tf_op jit(solution)/shard_map/ppermute | solution.py:19
  108.2 2.2 %collective-permute-done.5 = f32[12800]{0:T(1024)S(1)} collective-permute-done((f32[12800]{0:T(1024)S(1)}, f32[12800]{0:T(1024)S(1)}, u32[]{:S(2)}, u32[]{:S(2)}) %collective-permute-start.5) | collective-permute-done | bytes 51232 | tf_op jit(solution)/shard_map/ppermute | solution.py:19
  110.4 0.1 broadcast_in_dim.4
  110.6 9.5 %all_to_all.22 = f32[4,1,12800]{2,1,0:T(1,128)S(1)} all-to-all(f32[4,1,12800]{2,1,0:T(1,128)S(1)} %broadcast_in_dim.4), channel_id=1, replica_groups=mesh['zh'=3,'zl'=4,'core'=2,'y'=8,'x'=4] {'zl'}, dimensions={0} | all-to-all | bytes 409600 | tf_op jit(solution)/shard_map/all_to_all | solution.py:24
  120.1 0.8 reduce_sum.88
  120.9 1.6 broadcast_in_dim.5
  122.5 5.2 %all-to-all-start.3 = ((f32[3,1,12800]{2,1,0:T(1,128)}), f32[3,1,12800]{2,1,0:T(1,128)S(1)}, u32[]{:S(2)}, u32[]{:S(2)}) async-start(f32[3,1,12800]{2,1,0:T(1,128)} %broadcast_in_dim.5), calls=%async_computation.3 | async-start | bytes 307200 | tf_op jit(solution)/shard_map/all_to_all | solution.py:24
  127.7 2.4 %convolution_convert_fusion = bf16[48,12800]{1,0:T(8,128)(2,1)} fusion(f32[32,12800]{1,0:T(8,128)S(1)} %reshape.98, f32[12800]{0:T(1024)} %param.8, f32[12800]{0:T(1024)S(1)} %copy-done.1, f32[32]{0:T(128)S(1)} %rsqrt.12, f32[32]{0:T(128)S(1)} %div.15, s32[32]{0:T(128)S(1)} %multiply_add_fusion), kind=kOutput, calls=%fused_computation | convolution fusion | flops 41985536 | bytes 2969984 | tf_op jit(solution)/shard_map/dot_general | solution.py:85
  130.1 2.4 %reshape.92 = bf16[24,2,12800]{2,1,0:T(2,128)(2,1)} reshape(bf16[48,12800]{1,0:T(8,128)(2,1)} %convolution_convert_fusion) | data formatting | bytes 2457600 | tf_op jit(solution)/shard_map/reshape | solution.py:88
  132.4 5.1 %all-to-all-done.3 = f32[3,1,12800]{2,1,0:T(1,128)S(1)} async-done(((f32[3,1,12800]{2,1,0:T(1,128)}), f32[3,1,12800]{2,1,0:T(1,128)S(1)}, u32[]{:S(2)}, u32[]{:S(2)}) %all-to-all-start.3) | async-done | bytes 153632 | tf_op jit(solution)/shard_map/all_to_all | solution.py:24
  137.5 4.6 %all-to-all-start = ((bf16[24,2,12800]{2,1,0:T(2,128)(2,1)}), bf16[24,2,12800]{2,1,0:T(2,128)(2,1)}, u32[]{:S(2)}, u32[]{:S(2)}) async-start(bf16[24,2,12800]{2,1,0:T(2,128)(2,1)} %reshape.92), calls=%async_computation | async-start | bytes 2457600 | tf_op jit(solution)/shard_map/all_to_all | solution.py:89
  142.2 0.8 reduce_sum.89
  143.0 2.1 %collective-permute-start.6 = (f32[12800]{0:T(1024)}, f32[12800]{0:T(1024)S(1)}, u32[]{:S(2)}, u32[]{:S(2)}) collective-permute-start(f32[12800]{0:T(1024)} %reduce_sum.89), channel_id=1, source_target_pairs={{0,32},{32,0},{1,33},{33,1},{2,34},{34,2},{3,35},{35,3},{4,36},{36... | collective-permute-start | bytes 153608 | tf_op jit(solution)/shard_map/ppermute | solution.py:19
  145.1 1.4 multiply_convert_fusion
  146.5 2.3 %reshape.96 = bf16[2,16,2,2,3200]{4,3,2,1,0:T(2,128)(2,1)S(1)} reshape(bf16[32,12800]{1,0:T(8,128)(2,1)} %multiply_convert_fusion) | data formatting | bytes 1638400 | tf_op jit(solution)/shard_map/reshape | solution.py:49
  148.8 0.6 copy.14
  149.4 0.0 copy-start.2
  149.4 1.2 reshape.97
  150.6 38.5 %all-to-all-done = bf16[24,2,12800]{2,1,0:T(2,128)(2,1)} async-done(((bf16[24,2,12800]{2,1,0:T(2,128)(2,1)}), bf16[24,2,12800]{2,1,0:T(2,128)(2,1)}, u32[]{:S(2)}, u32[]{:S(2)}) %all-to-all-start) | async-done | bytes 1228832 | tf_op jit(solution)/shard_map/all_to_all | solution.py:89
  189.1 2.4 %reshape.93 = bf16[48,12800]{1,0:T(8,128)(2,1)} reshape(bf16[24,2,12800]{2,1,0:T(2,128)(2,1)} %all-to-all-done) | data formatting | bytes 2457600 | tf_op jit(solution)/shard_map/reshape | solution.py:90
  191.5 0.0 collective-permute-done.6
  191.5 0.7 select_multiply_fusion
  (17 shorter events, 0.1 us)
Async XLA Ops:
  3.0 15.6 %copy-start = (bf16[4,32,3200]{2,1,0:T(8,128)(2,1)S(1)}, bf16[4,32,3200]{2,1,0:T(8,128)(2,1)}, u32[]{:S(2)}) copy-start(bf16[4,32,3200]{2,1,0:T(8,128)(2,1)} %param.5) | copy-start | bytes 2457604
  3.0 62.5 %all-to-all-start.1 = ((bf16[24,2,12800]{2,1,0:T(2,128)(2,1)}), bf16[24,2,12800]{2,1,0:T(2,128)(2,1)}, u32[]{:S(2)}, u32[]{:S(2)}) async-start(bf16[24,2,12800]{2,1,0:T(2,128)(2,1)} %reshape.94), calls=%async_computation.1 | async-start | bytes 2457600 | tf_op jit(solution)/shard_map/all_to_all | solution.py:92
  21.2 1.3 copy-start.3
  22.6 45.3 %copy-start.1 = (f32[12800]{0:T(1024)S(1)}, f32[12800]{0:T(1024)}, u32[]{:S(2)}) copy-start(f32[12800]{0:T(1024)} %param.7) | copy-start | bytes 153604
  70.2 3.1 %collective-permute-start = (f32[12800]{0:T(1024)S(1)}, f32[12800]{0:T(1024)S(1)}, u32[]{:S(2)}, u32[]{:S(2)}) collective-permute-start(f32[12800]{0:T(1024)S(1)} %broadcast_select_fusion), channel_id=1, source_target_pairs={{0,32},{32,0},{1,33},{33,1},{2,34},{34,2},{3,35},{35,3},{4,36},{36... | collective-permute-start | bytes 153608 | tf_op jit(solution)/shard_map/ppermute | solution.py:19
  73.3 6.0 %collective-permute-start.1 = (f32[12800]{0:T(1024)S(1)}, f32[12800]{0:T(1024)S(1)}, u32[]{:S(2)}, u32[]{:S(2)}) collective-permute-start(f32[12800]{0:T(1024)S(1)} %select_add_fusion), channel_id=1, source_target_pairs={{0,1},{1,0},{2,3},{3,2},{4,5},{5,4},{6,7},{7,6},{8,9},{9,8},{10,11... | collective-permute-start | bytes 153608 | tf_op jit(solution)/shard_map/ppermute | solution.py:19
  79.3 7.5 %collective-permute-start.2 = (f32[12800]{0:T(1024)S(1)}, f32[12800]{0:T(1024)S(1)}, u32[]{:S(2)}, u32[]{:S(2)}) collective-permute-start(f32[12800]{0:T(1024)S(1)} %add.51), channel_id=1, source_target_pairs={{0,2},{1,3},{2,0},{3,1},{4,6},{5,7},{6,4},{7,5},{8,10},{9,11},{10,... | collective-permute-start | bytes 153608 | tf_op jit(solution)/shard_map/ppermute | solution.py:19
  86.9 6.0 %collective-permute-start.3 = (f32[12800]{0:T(1024)S(1)}, f32[12800]{0:T(1024)S(1)}, u32[]{:S(2)}, u32[]{:S(2)}) collective-permute-start(f32[12800]{0:T(1024)S(1)} %add.52), channel_id=1, source_target_pairs={{0,4},{4,0},{8,12},{12,8},{16,20},{20,16},{24,28},{28,24},{1,5},{5... | collective-permute-start | bytes 153608 | tf_op jit(solution)/shard_map/ppermute | solution.py:19
  92.9 6.9 %collective-permute-start.4 = (f32[12800]{0:T(1024)S(1)}, f32[12800]{0:T(1024)S(1)}, u32[]{:S(2)}, u32[]{:S(2)}) collective-permute-start(f32[12800]{0:T(1024)S(1)} %add.53), channel_id=1, source_target_pairs={{0,8},{4,12},{8,0},{12,4},{16,24},{20,28},{24,16},{28,20},{1,9},{5... | collective-permute-start | bytes 153608 | tf_op jit(solution)/shard_map/ppermute | solution.py:19
  99.9 10.6 %collective-permute-start.5 = (f32[12800]{0:T(1024)S(1)}, f32[12800]{0:T(1024)S(1)}, u32[]{:S(2)}, u32[]{:S(2)}) collective-permute-start(f32[12800]{0:T(1024)S(1)} %add.54), channel_id=1, source_target_pairs={{0,16},{4,20},{8,24},{12,28},{16,0},{20,4},{24,8},{28,12},{1,17},{... | collective-permute-start | bytes 153608 | tf_op jit(solution)/shard_map/ppermute | solution.py:19
  122.5 15.1 %all-to-all-start.3 = ((f32[3,1,12800]{2,1,0:T(1,128)}), f32[3,1,12800]{2,1,0:T(1,128)S(1)}, u32[]{:S(2)}, u32[]{:S(2)}) async-start(f32[3,1,12800]{2,1,0:T(1,128)} %broadcast_in_dim.5), calls=%async_computation.3 | async-start | bytes 307200 | tf_op jit(solution)/shard_map/all_to_all | solution.py:24
  137.5 51.5 %all-to-all-start = ((bf16[24,2,12800]{2,1,0:T(2,128)(2,1)}), bf16[24,2,12800]{2,1,0:T(2,128)(2,1)}, u32[]{:S(2)}, u32[]{:S(2)}) async-start(bf16[24,2,12800]{2,1,0:T(2,128)(2,1)} %reshape.92), calls=%async_computation | async-start | bytes 2457600 | tf_op jit(solution)/shard_map/all_to_all | solution.py:89
  143.0 48.4 %collective-permute-start.6 = (f32[12800]{0:T(1024)}, f32[12800]{0:T(1024)S(1)}, u32[]{:S(2)}, u32[]{:S(2)}) collective-permute-start(f32[12800]{0:T(1024)} %reduce_sum.89), channel_id=1, source_target_pairs={{0,32},{32,0},{1,33},{33,1},{2,34},{34,2},{3,35},{35,3},{4,36},{36... | collective-permute-start | bytes 153608 | tf_op jit(solution)/shard_map/ppermute | solution.py:19
  149.4 42.1 %copy-start.2 = (f32[12800]{0:T(1024)S(1)}, f32[12800]{0:T(1024)}, u32[]{:S(2)}) copy-start(f32[12800]{0:T(1024)} %reduce_sum.89) | copy-start | bytes 153604

commit v3 on v2

--- a/solution.py
+++ b/solution.py
@@ -9,9 +9,11 @@
 
 
 epsilon = 1e-05
-ENC = ("zh", "zl", "core")
+ENC = ("z", "core")
 REP = ("y", "x")
 EACH = ENC + REP
+FAR = (6, 5, 7, 4, 8)
+NEAR = (3, 9, 2, 10, 1, 11)
 
 
 def swapped(value, axis, flip):
@@ -19,24 +21,61 @@
     return lax.ppermute(value, axis, [(i, i ^ flip) for i in range(size)])
 
 
-def of_everyone(value, axis):
-    copies = jnp.broadcast_to(value, (lax.axis_size(axis), *value.shape))
-    everything = lax.all_to_all(copies, axis, split_axis=0, concat_axis=0, tiled=True)
-    return jnp.sum(everything, axis=0)
+def shifted(value, axis, by):
+    size = lax.axis_size(axis)
+    return lax.ppermute(value, axis, [(i, (i + by) % size) for i in range(size)])
+
+
+def exchanged(value, axis):
+    return lax.all_to_all(value, axis, split_axis=0, concat_axis=0, tiled=True)
+
+
+def to_everyone(value, axis):
+    return exchanged(jnp.broadcast_to(value, (lax.axis_size(axis), *value.shape)), axis)
 
 
 def total_of(gain_part, bias_part):
-    first = lax.axis_index("core") == 0
-    mine = jnp.where(first, gain_part, bias_part)
-    other = jnp.where(first, bias_part, gain_part)
-    total = mine + swapped(other, "core", 1)
-    for axis, flips in (("x", (1, 2)), ("y", (1, 2, 4))):
-        for flip in flips:
-            total = total + swapped(total, axis, flip)
-    for axis in ("zl", "zh"):
-        total = of_everyone(total, axis)
-    back = swapped(total, "core", 1)
-    return jnp.where(first, total, back), jnp.where(first, back, total)
+    pieces = jnp.concatenate([gain_part, bias_part]).reshape(lax.axis_size(REP), -1)
+    total = jnp.sum(exchanged(pieces, REP), axis=0)
+    total = jnp.sum(to_everyone(total, ENC), axis=0)
+    whole = to_everyone(total, REP).reshape(2, -1)
+    return whole[0], whole[1]
+
+
+def one_hot_rows(wanted, have):
+    return (wanted[:, None] == have[None, :]).astype(jnp.bfloat16)
+
+
+def picked(selector, rows):
+    return jnp.dot(selector, rows, preferred_element_type=jnp.float32).astype(jnp.bfloat16)
+
+
+def delivered(output, places, capacity):
+    deep, cores = lax.axis_size("z"), lax.axis_size("core")
+    z, core = lax.axis_index("z"), lax.axis_index("core")
+    wide = cores * capacity
+    row = jnp.arange(deep * capacity, dtype=jnp.int32)
+    target = (z + row // capacity) % deep * wide + row % capacity
+    target = jnp.concatenate([target + core * capacity, target + (1 - core) * capacity])
+    own, other = jnp.split(picked(one_hot_rows(target, places), output), 2)
+    met = swapped(other, "core", 1)
+    first = core == 0
+    rows = jnp.where(first, own, met), jnp.where(first, met, own)
+
+    def block(by):
+        cut = slice(by * capacity, (by + 1) * capacity)
+        return jnp.concatenate([half[cut] for half in rows])
+
+    came = {0: block(0)}
+    for group in (FAR, NEAR):
+        rows = lax.optimization_barrier(rows)
+        for by in group:
+            piece = block(by)
+            came[by] = shifted(piece, "z", by)
+    joined = jnp.concatenate([came[-j % deep] for j in range(deep)])
+    slot = jnp.arange(deep * wide, dtype=jnp.int32)
+    source = (slot // wide - z) % deep * wide + slot % wide
+    return picked(one_hot_rows(source, slot), joined)
 
 
 def shuffle_tokens(patches):
@@ -55,8 +94,8 @@
     center = jnp.mean(values, axis=-1, keepdims=True)
     spread = jnp.mean(jnp.square(values - center), axis=-1, keepdims=True)
     inverse = lax.rsqrt(spread + epsilon)
-    normed = (values - center) * inverse
-    return (normed, inverse, normed * norm_gain + norm_bias)
+    output = (values - center) * inverse * norm_gain + norm_bias
+    return (values, center, inverse, output)
 
 
 def norm_backward(upstream, normed, inverse, norm_gain):
@@ -78,18 +117,15 @@
     onehot = (owners[:, None] == jnp.arange(groups, dtype=jnp.int32)[None, :]).astype(jnp.int32)
     before = jnp.cumsum(onehot, axis=0) - onehot
     places = owners * capacity + jnp.sum(before * onehot, axis=1)
-    placer = (jnp.arange(groups * capacity, dtype=jnp.int32)[:, None] == places[None, :]).astype(
-        jnp.bfloat16
-    )
-    normed, inverse, output = norm_forward(tokens, norm_gain, norm_bias)
-    outgoing = jnp.dot(
-        placer, output.astype(jnp.bfloat16), preferred_element_type=jnp.float32
-    ).astype(jnp.bfloat16)
-    outgoing = outgoing.reshape(groups, capacity, feature_width)
-    arrived = lax.all_to_all(outgoing, ENC, split_axis=0, concat_axis=0, tiled=True)
-    visual = arrived.reshape(groups * capacity, feature_width)
+    placer = one_hot_rows(jnp.arange(groups * capacity, dtype=jnp.int32), places)
+    values, center, inverse, output = norm_forward(tokens, norm_gain, norm_bias)
+    visual = delivered(output.astype(jnp.bfloat16), places, capacity)
     slots = cotangent.reshape(groups, capacity, feature_width)
     returned = lax.all_to_all(slots, ENC, split_axis=0, concat_axis=0, tiled=True)
+    returned, values, center, inverse = lax.optimization_barrier(
+        (returned, values, center, inverse)
+    )
+    normed = (values - center) * inverse
     upstream = jnp.dot(
         placer.T,
         returned.reshape(groups * capacity, feature_width),
@@ -106,7 +142,7 @@
 
 def solution(mesh):
     placed = (P(EACH, None, None), P(EACH, None), P(), P(), P(EACH, None))
-    fine = Mesh(np.asarray(mesh.devices).reshape(3, 4, 2, 8, 4), EACH)
+    fine = Mesh(np.asarray(mesh.devices).reshape(12, 2, 8, 4), EACH)
     return jax.shard_map(
         steps,
         mesh=fine,

time: 193 us -> 190 us (0.984)
  waiting for transfers between devices: 102 us -> 60.2 us
  starting transfers between devices: 51.8 us -> 91.6 us
  blocking collectives: 9.52 us -> 0 us
  local copies, waits for them, and re-layouts: 17.7 us -> 24 us
    ppermute x0 -> x11, starting transfers between devices: none -> 51.8 us  [shifted(): lax.ppermute(value, axis, [(i, (i + by) % size) for i in range(size)])]
    all_to_all x1, waiting for transfers between devices: 42.6 us -> 0.01 us  [steps(): lax.all_to_all(slots, ENC, split_axis=0, concat_axis=0, tiled=True)]
    ppermute x0 -> x11, waiting for transfers between devices: none -> 39.5 us  [shifted(): lax.ppermute(value, axis, [(i, (i + by) % size) for i in range(size)])]
    ppermute x7 -> x1, starting transfers between devices: 26.4 us -> 1.91 us  [swapped(): return lax.ppermute(value, axis, [(i, i ^ flip) for i in range(size)])]
    all_to_all x2 -> x3, waiting for transfers between devices: 43.6 us -> 20.7 us  [exchanged(): return lax.all_to_all(value, axis, split_axis=0, concat_axis=0, tiled=True)]
    ppermute x7 -> x1, waiting for transfers between devices: 15.9 us -> 0.01 us  [swapped(): return lax.ppermute(value, axis, [(i, i ^ flip) for i in range(size)])]
    all_to_all x2 -> x3, starting transfers between devices: 9.85 us -> 22.3 us  [exchanged(): return lax.all_to_all(value, axis, split_axis=0, concat_axis=0, tiled=True)]
    all_to_all x1 -> x0, blocking collectives: 9.52 us -> none  [of_everyone(): lax.all_to_all(copies, axis, split_axis=0, concat_axis=0, tiled=True)]
  transfers between devices with their start and end apart: 10 -> 16, of which waited for: 9 -> 7; matrix products, arithmetic and copies ran while one was open for 9% -> 10% of each run, Pallas kernels for 0% -> 0%
where the time goes in v3:
time: 190 us; the launch traced here: 188 us
  starting transfers between devices  91.6 us (48%)
  waiting for transfers between devices  60.2 us (32%)
  local copies, waits for them, and re-layouts  24 us (13%)
  other arithmetic  5.94 us (3%)
  matrix products  5.64 us (3%)
    ppermute x11, starting transfers between devices, shifted(): lax.ppermute(value, axis, [(i, (i + by) % size) for i in range(size)])  51.8 us
    ppermute x11, waiting for transfers between devices, shifted(): lax.ppermute(value, axis, [(i, (i + by) % size) for i in range(size)])  39.5 us
    all_to_all x3, starting transfers between devices, exchanged(): return lax.all_to_all(value, axis, split_axis=0, concat_axis=0, tiled=True)  22.3 us
    all_to_all x3, waiting for transfers between devices, exchanged(): return lax.all_to_all(value, axis, split_axis=0, concat_axis=0, tiled=True)  20.7 us
    all_to_all x1, starting transfers between devices, steps(): lax.all_to_all(slots, ENC, split_axis=0, concat_axis=0, tiled=True)  15.6 us
    concatenate x1, local copies, waits for them, and re-layouts, delivered(): joined = jnp.concatenate([came[-j % deep] for j in range(deep)])  5 us
  transfers between devices with their start and end apart: 16, of which 7 were waited for; matrix products, arithmetic and copies ran while one was open for 10% of the time, Pallas kernels for 0%

profile of v3, /device:TPU:6, one launch (start us, length us, event | category | flops | bytes accessed | tf_op | source)
XLA Modules:
  0.0 188.4 jit_solution(53470610989884022)
XLA Ops:
  0.6 2.2 %reshape.163 = f32[2,2,16,2,3200]{4,3,2,1,0:T(2,128)S(1)} reshape(bf16[4,32,3200]{2,1,0:T(8,128)(2,1)} %param.5) | data formatting | bytes 2457600 | tf_op jit(solution)/shard_map/convert_element_type | solution.py:93
  2.9 0.4 fusion.21
  3.4 1.0 multiply_reduce_fusion.2
  4.6 1.3 reshape.161
  6.4 0.6 convolution_convert_fusion.1
  7.0 0.9 split.9
  7.9 1.9 %collective-permute-start = (bf16[24,12800]{1,0:T(8,128)(2,1)}, bf16[24,12800]{1,0:T(8,128)(2,1)S(1)}, u32[]{:S(2)}, u32[]{:S(2)}) collective-permute-start(bf16[24,12800]{1,0:T(8,128)(2,1)} %split.9), channel_id=1, source_target_pairs={{0,32},{32,0},{1,33},{33,1},{2,34},{34,2},{3,35},{35,3},{4,36},{36... | collective-permute-start | bytes 1843208 | tf_op jit(solution)/shard_map/ppermute | solution.py:21
  9.8 2.4 %reshape.157 = bf16[24,2,12800]{2,1,0:T(2,128)(2,1)} reshape(bf16[48,12800]{1,0:T(8,128)(2,1)} %param.9) | data formatting | bytes 2457600 | tf_op jit(solution)/shard_map/reshape | solution.py:123
  12.2 15.6 %all-to-all-start = ((bf16[24,2,12800]{2,1,0:T(2,128)(2,1)}), bf16[24,2,12800]{2,1,0:T(2,128)(2,1)}, u32[]{:S(2)}, u32[]{:S(2)}) async-start(bf16[24,2,12800]{2,1,0:T(2,128)(2,1)} %reshape.157), calls=%async_computation | async-start | bytes 2457600 | tf_op jit(solution)/shard_map/all_to_all | solution.py:124
  28.0 0.3 fusion.22
  28.3 0.3 fusion.23
  28.6 3.7 %collective-permute-start.11 = (bf16[4,12800]{1,0:T(4,128)(2,1)S(1)}, bf16[4,12800]{1,0:T(4,128)(2,1)S(1)}, u32[]{:S(2)}, u32[]{:S(2)}) collective-permute-start(bf16[4,12800]{1,0:T(4,128)(2,1)S(1)} %pad_maximum_fusion.11), channel_id=1, source_target_pairs={{0,64},{64,128},{128,192},{192,256},{256,320},{320,384},{384,448},... | collective-permute-start | bytes 307208 | tf_op jit(solution)/shard_map/ppermute | solution.py:26
  32.5 4.3 %collective-permute-start.10 = (bf16[4,12800]{1,0:T(4,128)(2,1)S(1)}, bf16[4,12800]{1,0:T(4,128)(2,1)S(1)}, u32[]{:S(2)}, u32[]{:S(2)}) collective-permute-start(bf16[4,12800]{1,0:T(4,128)(2,1)S(1)} %pad_maximum_fusion.10), channel_id=1, source_target_pairs={{0,128},{64,192},{128,256},{192,320},{256,384},{320,448},{384,512}... | collective-permute-start | bytes 307208 | tf_op jit(solution)/shard_map/ppermute | solution.py:26
  36.9 6.4 %collective-permute-start.9 = (bf16[4,12800]{1,0:T(4,128)(2,1)S(1)}, bf16[4,12800]{1,0:T(4,128)(2,1)S(1)}, u32[]{:S(2)}, u32[]{:S(2)}) collective-permute-start(bf16[4,12800]{1,0:T(4,128)(2,1)S(1)} %pad_maximum_fusion.9), channel_id=1, source_target_pairs={{0,192},{64,256},{128,320},{192,384},{256,448},{320,512},{384,576}... | collective-permute-start | bytes 307208 | tf_op jit(solution)/shard_map/ppermute | solution.py:26
  43.7 3.1 %collective-permute-start.8 = (bf16[4,12800]{1,0:T(4,128)(2,1)S(1)}, bf16[4,12800]{1,0:T(4,128)(2,1)S(1)}, u32[]{:S(2)}, u32[]{:S(2)}) collective-permute-start(bf16[4,12800]{1,0:T(4,128)(2,1)S(1)} %pad_maximum_fusion.8), channel_id=1, source_target_pairs={{0,256},{64,320},{128,384},{192,448},{256,512},{320,576},{384,640}... | collective-permute-start | bytes 307208 | tf_op jit(solution)/shard_map/ppermute | solution.py:26
  47.0 5.2 %collective-permute-start.7 = (bf16[4,12800]{1,0:T(4,128)(2,1)S(1)}, bf16[4,12800]{1,0:T(4,128)(2,1)S(1)}, u32[]{:S(2)}, u32[]{:S(2)}) collective-permute-start(bf16[4,12800]{1,0:T(4,128)(2,1)S(1)} %pad_maximum_fusion.7), channel_id=1, source_target_pairs={{0,320},{64,384},{128,448},{192,512},{256,576},{320,640},{384,704}... | collective-permute-start | bytes 307208 | tf_op jit(solution)/shard_map/ppermute | solution.py:26
  52.7 21.6 %collective-permute-done.11 = bf16[4,12800]{1,0:T(4,128)(2,1)S(1)} collective-permute-done((bf16[4,12800]{1,0:T(4,128)(2,1)S(1)}, bf16[4,12800]{1,0:T(4,128)(2,1)S(1)}, u32[]{:S(2)}, u32[]{:S(2)}) %collective-permute-start.11) | collective-permute-done | bytes 102432 | tf_op jit(solution)/shard_map/ppermute | solution.py:26
  74.3 6.8 %collective-permute-start.6 = (bf16[4,12800]{1,0:T(4,128)(2,1)S(1)}, bf16[4,12800]{1,0:T(4,128)(2,1)S(1)}, u32[]{:S(2)}, u32[]{:S(2)}) collective-permute-start(bf16[4,12800]{1,0:T(4,128)(2,1)S(1)} %pad_maximum_fusion.6), channel_id=1, source_target_pairs={{0,384},{64,448},{128,512},{192,576},{256,640},{320,704},{384,0},{... | collective-permute-start | bytes 307208 | tf_op jit(solution)/shard_map/ppermute | solution.py:26
  81.3 4.8 %collective-permute-start.5 = (bf16[4,12800]{1,0:T(4,128)(2,1)S(1)}, bf16[4,12800]{1,0:T(4,128)(2,1)S(1)}, u32[]{:S(2)}, u32[]{:S(2)}) collective-permute-start(bf16[4,12800]{1,0:T(4,128)(2,1)S(1)} %pad_maximum_fusion.5), channel_id=1, source_target_pairs={{0,448},{64,512},{128,576},{192,640},{256,704},{320,0},{384,64},{4... | collective-permute-start | bytes 307208 | tf_op jit(solution)/shard_map/ppermute | solution.py:26
  86.0 7.7 %collective-permute-start.4 = (bf16[4,12800]{1,0:T(4,128)(2,1)S(1)}, bf16[4,12800]{1,0:T(4,128)(2,1)S(1)}, u32[]{:S(2)}, u32[]{:S(2)}) collective-permute-start(bf16[4,12800]{1,0:T(4,128)(2,1)S(1)} %pad_maximum_fusion.4), channel_id=1, source_target_pairs={{0,512},{64,576},{128,640},{192,704},{256,0},{320,64},{384,128},{4... | collective-permute-start | bytes 307208 | tf_op jit(solution)/shard_map/ppermute | solution.py:26
  93.7 6.1 %collective-permute-start.3 = (bf16[4,12800]{1,0:T(4,128)(2,1)S(1)}, bf16[4,12800]{1,0:T(4,128)(2,1)S(1)}, u32[]{:S(2)}, u32[]{:S(2)}) collective-permute-start(bf16[4,12800]{1,0:T(4,128)(2,1)S(1)} %pad_maximum_fusion.3), channel_id=1, source_target_pairs={{0,576},{64,640},{128,704},{192,0},{256,64},{320,128},{384,192},{4... | collective-permute-start | bytes 307208 | tf_op jit(solution)/shard_map/ppermute | solution.py:26
  99.8 12.0 %collective-permute-done.7 = bf16[4,12800]{1,0:T(4,128)(2,1)S(1)} collective-permute-done((bf16[4,12800]{1,0:T(4,128)(2,1)S(1)}, bf16[4,12800]{1,0:T(4,128)(2,1)S(1)}, u32[]{:S(2)}, u32[]{:S(2)}) %collective-permute-start.7) | collective-permute-done | bytes 102432 | tf_op jit(solution)/shard_map/ppermute | solution.py:26
  111.8 1.9 %collective-permute-start.2 = (bf16[4,12800]{1,0:T(4,128)(2,1)S(1)}, bf16[4,12800]{1,0:T(4,128)(2,1)S(1)}, u32[]{:S(2)}, u32[]{:S(2)}) collective-permute-start(bf16[4,12800]{1,0:T(4,128)(2,1)S(1)} %pad_maximum_fusion.2), channel_id=1, source_target_pairs={{0,640},{64,704},{128,0},{192,64},{256,128},{320,192},{384,256},{4... | collective-permute-start | bytes 307208 | tf_op jit(solution)/shard_map/ppermute | solution.py:26
  113.7 1.9 %collective-permute-start.1 = (bf16[4,12800]{1,0:T(4,128)(2,1)S(1)}, bf16[4,12800]{1,0:T(4,128)(2,1)S(1)}, u32[]{:S(2)}, u32[]{:S(2)}) collective-permute-start(bf16[4,12800]{1,0:T(4,128)(2,1)S(1)} %pad_maximum_fusion.1), channel_id=1, source_target_pairs={{0,704},{64,0},{128,64},{192,128},{256,192},{320,256},{384,320},{4... | collective-permute-start | bytes 307208 | tf_op jit(solution)/shard_map/ppermute | solution.py:26
  115.8 4.6 %collective-permute-done.2 = bf16[4,12800]{1,0:T(4,128)(2,1)S(1)} collective-permute-done((bf16[4,12800]{1,0:T(4,128)(2,1)S(1)}, bf16[4,12800]{1,0:T(4,128)(2,1)S(1)}, u32[]{:S(2)}, u32[]{:S(2)}) %collective-permute-start.2) | collective-permute-done | bytes 102432 | tf_op jit(solution)/shard_map/ppermute | solution.py:26
  120.4 1.3 collective-permute-done.1
  121.7 5.0 %concatenate.59 = bf16[48,12800]{1,0:T(8,128)(2,1)} concatenate(bf16[2,12800]{1,0:T(2,128)(2,1)S(1)} %slice.108, bf16[2,12800]{1,0:T(2,128)(2,1)S(1)} %slice.109, bf16[4,12800]{1,0:T(4,128)(2,1)S(1)} %collective-permute-done.1, bf16[4,12800]{1,0:T(4,128)(2,1)S(1)} %collective-permute-done.2, bf16[4,12800]{1,0:T(4,128)(2,1)S(1)} %collective-permute-done.3, ...), dimensions={0} | concatenate | bytes 2457600 | tf_op jit(solution)/shard_map/concatenate | solution.py:75
  126.7 2.4 %reshape.158 = bf16[48,12800]{1,0:T(8,128)(2,1)} reshape(bf16[24,2,12800]{2,1,0:T(2,128)(2,1)} %all-to-all-done) | data formatting | bytes 2457600 | tf_op jit(solution)/shard_map/reshape | solution.py:131
  129.1 2.3 %multiply_reduce_fusion = (f32[12800]{0:T(1024)S(1)}, f32[32]{0:T(128)S(1)}, f32[32]{0:T(128)S(1)}, f32[12800]{0:T(1024)S(1)}, f32[32,12800]{1,0:T(8,128)S(1)}) fusion(f32[32,12800]{1,0:T(8,128)S(1)} %reshape.161, f32[32]{0:T(128)S(1)} %bitcast.20, f32[32]{0:T(128)S(1)} %bitcast.18, f32[12800]{0:T(1024)S(1)} %copy-done, bf16[48,12800]{1,0:T(8,128)(2,1)} %reshape.158, ...), kind=kOutput, calls=%fused_computation.3 | convolution fusion | flops 42983872 | bytes 4659840 | tf_op jit(solution)/shard_map/dot_general | solution.py:129
  131.4 0.7 concatenate.61
  132.1 0.8 pad_maximum_fusion
  133.0 0.7 all_to_all.18
  133.7 10.2 %all-to-all-start.1 = ((f32[32,1,800]{2,1,0:T(1,128)}), f32[32,1,800]{2,1,0:T(1,128)S(1)}, u32[]{:S(2)}, u32[]{:S(2)}) async-start(f32[32,1,800]{2,1,0:T(1,128)} %all_to_all.18), calls=%async_computation.1 | async-start | bytes 229376 | tf_op jit(solution)/shard_map/all_to_all | solution.py:30
  143.9 2.8 %convolution_convert_fusion = bf16[48,12800]{1,0:T(8,128)(2,1)} fusion(bf16[48,12800]{1,0:T(8,128)(2,1)} %concatenate.59, s32[48]{0:T(128)S(1)} %fusion.13), kind=kOutput, calls=%fused_computation | convolution fusion | flops 59599104 | bytes 2457792 | tf_op jit(solution)/shard_map/dot_general | solution.py:50
  146.7 6.0 %all-to-all-done.1 = f32[32,1,800]{2,1,0:T(1,128)S(1)} async-done(((f32[32,1,800]{2,1,0:T(1,128)}), f32[32,1,800]{2,1,0:T(1,128)S(1)}, u32[]{:S(2)}, u32[]{:S(2)}) %all-to-all-start.1) | async-done | bytes 102432 | tf_op jit(solution)/shard_map/all_to_all | solution.py:30
  152.8 0.7 broadcast_in_dim.4
  153.5 6.8 %all-to-all-start.2 = ((f32[24,1,800]{2,1,0:T(1,128)}), f32[24,1,800]{2,1,0:T(1,128)S(1)}, u32[]{:S(2)}, u32[]{:S(2)}) async-start(f32[24,1,800]{2,1,0:T(1,128)} %broadcast_in_dim.4), calls=%async_computation.2 | async-start | bytes 172032 | tf_op jit(solution)/shard_map/all_to_all | solution.py:30
  160.3 11.1 %all-to-all-done.2 = f32[24,1,800]{2,1,0:T(1,128)S(1)} async-done(((f32[24,1,800]{2,1,0:T(1,128)}), f32[24,1,800]{2,1,0:T(1,128)S(1)}, u32[]{:S(2)}, u32[]{:S(2)}) %all-to-all-start.2) | async-done | bytes 76832 | tf_op jit(solution)/shard_map/all_to_all | solution.py:30
  171.4 0.7 broadcast_in_dim.5
  172.1 5.4 %all-to-all-start.3 = ((f32[32,1,800]{2,1,0:T(1,128)}), f32[32,1,800]{2,1,0:T(1,128)S(1)}, u32[]{:S(2)}, u32[]{:S(2)}) async-start(f32[32,1,800]{2,1,0:T(1,128)} %broadcast_in_dim.5), calls=%async_computation.3 | async-start | bytes 229376 | tf_op jit(solution)/shard_map/all_to_all | solution.py:30
  177.5 1.4 multiply_convert_fusion
  178.8 2.3 %reshape.159 = bf16[2,16,2,2,3200]{4,3,2,1,0:T(2,128)(2,1)S(1)} reshape(bf16[32,12800]{1,0:T(8,128)(2,1)} %multiply_convert_fusion) | data formatting | bytes 1638400 | tf_op jit(solution)/shard_map/reshape | solution.py:88
  181.2 0.6 copy.16
  181.8 1.2 reshape.160
  183.0 3.6 %all-to-all-done.3 = f32[32,1,800]{2,1,0:T(1,128)S(1)} async-done(((f32[32,1,800]{2,1,0:T(1,128)}), f32[32,1,800]{2,1,0:T(1,128)S(1)}, u32[]{:S(2)}, u32[]{:S(2)}) %all-to-all-start.3) | async-done | bytes 102432 | tf_op jit(solution)/shard_map/all_to_all | solution.py:30
  186.6 0.3 fusion.4
  186.9 0.7 mul.115
  187.7 0.7 mul.117
  (49 shorter events, 2.9 us)
Async XLA Ops:
  4.6 1.3 copy-start.2
  4.6 1.9 copy-start
  4.6 1.9 copy-start.1
  7.9 20.0 %collective-permute-start = (bf16[24,12800]{1,0:T(8,128)(2,1)}, bf16[24,12800]{1,0:T(8,128)(2,1)S(1)}, u32[]{:S(2)}, u32[]{:S(2)}) collective-permute-start(bf16[24,12800]{1,0:T(8,128)(2,1)} %split.9), channel_id=1, source_target_pairs={{0,32},{32,0},{1,33},{33,1},{2,34},{34,2},{3,35},{35,3},{4,36},{36... | collective-permute-start | bytes 1843208 | tf_op jit(solution)/shard_map/ppermute | solution.py:21
  12.2 114.5 %all-to-all-start = ((bf16[24,2,12800]{2,1,0:T(2,128)(2,1)}), bf16[24,2,12800]{2,1,0:T(2,128)(2,1)}, u32[]{:S(2)}, u32[]{:S(2)}) async-start(bf16[24,2,12800]{2,1,0:T(2,128)(2,1)} %reshape.157), calls=%async_computation | async-start | bytes 2457600 | tf_op jit(solution)/shard_map/all_to_all | solution.py:124
  28.6 45.6 %collective-permute-start.11 = (bf16[4,12800]{1,0:T(4,128)(2,1)S(1)}, bf16[4,12800]{1,0:T(4,128)(2,1)S(1)}, u32[]{:S(2)}, u32[]{:S(2)}) collective-permute-start(bf16[4,12800]{1,0:T(4,128)(2,1)S(1)} %pad_maximum_fusion.11), channel_id=1, source_target_pairs={{0,64},{64,128},{128,192},{192,256},{256,320},{320,384},{384,448},... | collective-permute-start | bytes 307208 | tf_op jit(solution)/shard_map/ppermute | solution.py:26
  32.5 48.8 %collective-permute-start.10 = (bf16[4,12800]{1,0:T(4,128)(2,1)S(1)}, bf16[4,12800]{1,0:T(4,128)(2,1)S(1)}, u32[]{:S(2)}, u32[]{:S(2)}) collective-permute-start(bf16[4,12800]{1,0:T(4,128)(2,1)S(1)} %pad_maximum_fusion.10), channel_id=1, source_target_pairs={{0,128},{64,192},{128,256},{192,320},{256,384},{320,448},{384,512}... | collective-permute-start | bytes 307208 | tf_op jit(solution)/shard_map/ppermute | solution.py:26
  36.9 49.2 %collective-permute-start.9 = (bf16[4,12800]{1,0:T(4,128)(2,1)S(1)}, bf16[4,12800]{1,0:T(4,128)(2,1)S(1)}, u32[]{:S(2)}, u32[]{:S(2)}) collective-permute-start(bf16[4,12800]{1,0:T(4,128)(2,1)S(1)} %pad_maximum_fusion.9), channel_id=1, source_target_pairs={{0,192},{64,256},{128,320},{192,384},{256,448},{320,512},{384,576}... | collective-permute-start | bytes 307208 | tf_op jit(solution)/shard_map/ppermute | solution.py:26
  43.7 50.0 %collective-permute-start.8 = (bf16[4,12800]{1,0:T(4,128)(2,1)S(1)}, bf16[4,12800]{1,0:T(4,128)(2,1)S(1)}, u32[]{:S(2)}, u32[]{:S(2)}) collective-permute-start(bf16[4,12800]{1,0:T(4,128)(2,1)S(1)} %pad_maximum_fusion.8), channel_id=1, source_target_pairs={{0,256},{64,320},{128,384},{192,448},{256,512},{320,576},{384,640}... | collective-permute-start | bytes 307208 | tf_op jit(solution)/shard_map/ppermute | solution.py:26
  47.0 64.9 %collective-permute-start.7 = (bf16[4,12800]{1,0:T(4,128)(2,1)S(1)}, bf16[4,12800]{1,0:T(4,128)(2,1)S(1)}, u32[]{:S(2)}, u32[]{:S(2)}) collective-permute-start(bf16[4,12800]{1,0:T(4,128)(2,1)S(1)} %pad_maximum_fusion.7), channel_id=1, source_target_pairs={{0,320},{64,384},{128,448},{192,512},{256,576},{320,640},{384,704}... | collective-permute-start | bytes 307208 | tf_op jit(solution)/shard_map/ppermute | solution.py:26
  74.3 39.5 %collective-permute-start.6 = (bf16[4,12800]{1,0:T(4,128)(2,1)S(1)}, bf16[4,12800]{1,0:T(4,128)(2,1)S(1)}, u32[]{:S(2)}, u32[]{:S(2)}) collective-permute-start(bf16[4,12800]{1,0:T(4,128)(2,1)S(1)} %pad_maximum_fusion.6), channel_id=1, source_target_pairs={{0,384},{64,448},{128,512},{192,576},{256,640},{320,704},{384,0},{... | collective-permute-start | bytes 307208 | tf_op jit(solution)/shard_map/ppermute | solution.py:26
  81.3 34.5 %collective-permute-start.5 = (bf16[4,12800]{1,0:T(4,128)(2,1)S(1)}, bf16[4,12800]{1,0:T(4,128)(2,1)S(1)}, u32[]{:S(2)}, u32[]{:S(2)}) collective-permute-start(bf16[4,12800]{1,0:T(4,128)(2,1)S(1)} %pad_maximum_fusion.5), channel_id=1, source_target_pairs={{0,448},{64,512},{128,576},{192,640},{256,704},{320,0},{384,64},{4... | collective-permute-start | bytes 307208 | tf_op jit(solution)/shard_map/ppermute | solution.py:26
  86.0 29.8 %collective-permute-start.4 = (bf16[4,12800]{1,0:T(4,128)(2,1)S(1)}, bf16[4,12800]{1,0:T(4,128)(2,1)S(1)}, u32[]{:S(2)}, u32[]{:S(2)}) collective-permute-start(bf16[4,12800]{1,0:T(4,128)(2,1)S(1)} %pad_maximum_fusion.4), channel_id=1, source_target_pairs={{0,512},{64,576},{128,640},{192,704},{256,0},{320,64},{384,128},{4... | collective-permute-start | bytes 307208 | tf_op jit(solution)/shard_map/ppermute | solution.py:26
  93.7 22.1 %collective-permute-start.3 = (bf16[4,12800]{1,0:T(4,128)(2,1)S(1)}, bf16[4,12800]{1,0:T(4,128)(2,1)S(1)}, u32[]{:S(2)}, u32[]{:S(2)}) collective-permute-start(bf16[4,12800]{1,0:T(4,128)(2,1)S(1)} %pad_maximum_fusion.3), channel_id=1, source_target_pairs={{0,576},{64,640},{128,704},{192,0},{256,64},{320,128},{384,192},{4... | collective-permute-start | bytes 307208 | tf_op jit(solution)/shard_map/ppermute | solution.py:26
  111.8 8.5 %collective-permute-start.2 = (bf16[4,12800]{1,0:T(4,128)(2,1)S(1)}, bf16[4,12800]{1,0:T(4,128)(2,1)S(1)}, u32[]{:S(2)}, u32[]{:S(2)}) collective-permute-start(bf16[4,12800]{1,0:T(4,128)(2,1)S(1)} %pad_maximum_fusion.2), channel_id=1, source_target_pairs={{0,640},{64,704},{128,0},{192,64},{256,128},{320,192},{384,256},{4... | collective-permute-start | bytes 307208 | tf_op jit(solution)/shard_map/ppermute | solution.py:26
  113.7 8.0 %collective-permute-start.1 = (bf16[4,12800]{1,0:T(4,128)(2,1)S(1)}, bf16[4,12800]{1,0:T(4,128)(2,1)S(1)}, u32[]{:S(2)}, u32[]{:S(2)}) collective-permute-start(bf16[4,12800]{1,0:T(4,128)(2,1)S(1)} %pad_maximum_fusion.1), channel_id=1, source_target_pairs={{0,704},{64,0},{128,64},{192,128},{256,192},{320,256},{384,320},{4... | collective-permute-start | bytes 307208 | tf_op jit(solution)/shard_map/ppermute | solution.py:26
  133.7 19.0 %all-to-all-start.1 = ((f32[32,1,800]{2,1,0:T(1,128)}), f32[32,1,800]{2,1,0:T(1,128)S(1)}, u32[]{:S(2)}, u32[]{:S(2)}) async-start(f32[32,1,800]{2,1,0:T(1,128)} %all_to_all.18), calls=%async_computation.1 | async-start | bytes 229376 | tf_op jit(solution)/shard_map/all_to_all | solution.py:30
  153.5 17.9 %all-to-all-start.2 = ((f32[24,1,800]{2,1,0:T(1,128)}), f32[24,1,800]{2,1,0:T(1,128)S(1)}, u32[]{:S(2)}, u32[]{:S(2)}) async-start(f32[24,1,800]{2,1,0:T(1,128)} %broadcast_in_dim.4), calls=%async_computation.2 | async-start | bytes 172032 | tf_op jit(solution)/shard_map/all_to_all | solution.py:30
  172.1 14.5 %all-to-all-start.3 = ((f32[32,1,800]{2,1,0:T(1,128)}), f32[32,1,800]{2,1,0:T(1,128)S(1)}, u32[]{:S(2)}, u32[]{:S(2)}) async-start(f32[32,1,800]{2,1,0:T(1,128)} %broadcast_in_dim.5), calls=%async_computation.3 | async-start | bytes 229376 | tf_op jit(solution)/shard_map/all_to_all | solution.py:30

commit v4 on v3

--- a/solution.py
+++ b/solution.py
@@ -13,7 +13,8 @@
 REP = ("y", "x")
 EACH = ENC + REP
 FAR = (6, 5, 7, 4, 8)
-NEAR = (3, 9, 2, 10, 1, 11)
+MID = (1,)
+NEAR = (11, 10, 9, 3, 2)
 
 
 def swapped(value, axis, flip):
@@ -35,11 +36,14 @@
 
 
 def total_of(gain_part, bias_part):
-    pieces = jnp.concatenate([gain_part, bias_part]).reshape(lax.axis_size(REP), -1)
+    width, parts = gain_part.size, lax.axis_size(REP)
+    chunk = -(-2 * width // (1024 * parts)) * 1024
+    spare = jnp.zeros((parts * chunk - 2 * width,), jnp.float32)
+    pieces = jnp.concatenate([gain_part, bias_part, spare]).reshape(parts, chunk)
     total = jnp.sum(exchanged(pieces, REP), axis=0)
     total = jnp.sum(to_everyone(total, ENC), axis=0)
-    whole = to_everyone(total, REP).reshape(2, -1)
-    return whole[0], whole[1]
+    whole = to_everyone(total, REP).reshape(-1)
+    return whole[:width], whole[width : 2 * width]
 
 
 def one_hot_rows(wanted, have):
@@ -67,7 +71,8 @@
         return jnp.concatenate([half[cut] for half in rows])
 
     came = {0: block(0)}
-    for group in (FAR, NEAR):
+    plan = (FAR, MID, NEAR)
+    for group in plan:
         rows = lax.optimization_barrier(rows)
         for by in group:
             piece = block(by)
@@ -86,7 +91,8 @@
 
 def unshuffle_tokens(tokens, height, across, channels):
     grouped = tokens.reshape(height // 2, across // 2, 2, 2, channels)
-    return grouped.transpose(0, 2, 1, 3, 4).reshape(height, across, channels)
+    grouped = grouped.transpose(0, 2, 1, 3, 4)
+    return grouped.reshape(height, across, channels)
 
 
 def norm_forward(values, norm_gain, norm_bias):

time: 190 us -> 187 us (0.984)
  waiting for transfers between devices: 60.2 us -> 45.1 us
  other arithmetic: 5.94 us -> 14.5 us
  local copies, waits for them, and re-layouts: 24 us -> 29 us
  starting transfers between devices: 91.6 us -> 89.2 us
    ppermute x11, waiting for transfers between devices: 39.5 us -> 18.7 us  [shifted(): lax.ppermute(value, axis, [(i, (i + by) % size) for i in range(size)])]
    all_to_all x1, waiting for transfers between devices: 0.01 us -> 14.3 us  [steps(): lax.all_to_all(slots, ENC, split_axis=0, concat_axis=0, tiled=True)]
    all_to_all x3, waiting for transfers between devices: 20.7 us -> 12.1 us  [exchanged(): return lax.all_to_all(value, axis, split_axis=0, concat_axis=0, tiled=True)]
    concatenate x11, other arithmetic: 1.23 us -> 8.58 us  [block(): return jnp.concatenate([half[cut] for half in rows])]
    ppermute x11, starting transfers between devices: 51.8 us -> 46.5 us  [shifted(): lax.ppermute(value, axis, [(i, (i + by) % size) for i in range(size)])]
    concatenate x1, local copies, waits for them, and re-layouts: 5 us -> 9.79 us  [delivered(): joined = jnp.concatenate([came[-j % deep] for j in range(deep)])]
    slice x6 -> x8, local copies, waits for them, and re-layouts: 0.95 us -> 4.09 us  [block(): return jnp.concatenate([half[cut] for half in rows])]
    all_to_all x3, starting transfers between devices: 22.3 us -> 25.2 us  [exchanged(): return lax.all_to_all(value, axis, split_axis=0, concat_axis=0, tiled=True)]
  transfers between devices with their start and end apart: 16 -> 16, of which waited for: 7 -> 8; matrix products, arithmetic and copies ran while one was open for 10% -> 22% of each run, Pallas kernels for 0% -> 0%
where the time goes in v4:
time: 187 us; the launch traced here: 184 us
  starting transfers between devices  89.2 us (48%)
  waiting for transfers between devices  45.1 us (24%)
  local copies, waits for them, and re-layouts  29 us (16%)
  other arithmetic  14.5 us (8%)
  matrix products  5.63 us (3%)
    ppermute x11, starting transfers between devices, shifted(): lax.ppermute(value, axis, [(i, (i + by) % size) for i in range(size)])  46.5 us
    all_to_all x3, starting transfers between devices, exchanged(): return lax.all_to_all(value, axis, split_axis=0, concat_axis=0, tiled=True)  25.2 us
    ppermute x11, waiting for transfers between devices, shifted(): lax.ppermute(value, axis, [(i, (i + by) % size) for i in range(size)])  18.7 us
    all_to_all x1, starting transfers between devices, steps(): lax.all_to_all(slots, ENC, split_axis=0, concat_axis=0, tiled=True)  15.6 us
    all_to_all x1, waiting for transfers between devices, steps(): lax.all_to_all(slots, ENC, split_axis=0, concat_axis=0, tiled=True)  14.3 us
    all_to_all x3, waiting for transfers between devices, exchanged(): return lax.all_to_all(value, axis, split_axis=0, concat_axis=0, tiled=True)  12.1 us
    concatenate x1, local copies, waits for them, and re-layouts, delivered(): joined = jnp.concatenate([came[-j % deep] for j in range(deep)])  9.79 us
    concatenate x11, other arithmetic, block(): return jnp.concatenate([half[cut] for half in rows])  8.58 us
  transfers between devices with their start and end apart: 16, of which 8 were waited for; matrix products, arithmetic and copies ran while one was open for 22% of the time, Pallas kernels for 0%

profile of v4, /device:TPU:6, one launch (start us, length us, event | category | flops | bytes accessed | tf_op | source)
XLA Modules:
  0.0 184.4 jit_solution(1771564279910590148)
XLA Ops:
  0.6 2.2 %reshape.154 = f32[2,2,16,2,3200]{4,3,2,1,0:T(2,128)S(1)} reshape(bf16[4,32,3200]{2,1,0:T(8,128)(2,1)} %param.5) | data formatting | bytes 2457600 | tf_op jit(solution)/shard_map/convert_element_type | solution.py:99
  3.4 1.0 multiply_reduce_fusion.2
  4.6 1.3 reshape.152
  7.0 0.9 split.9
  7.9 1.9 %collective-permute-start = (bf16[24,12800]{1,0:T(8,128)(2,1)}, bf16[24,12800]{1,0:T(8,128)(2,1)}, u32[]{:S(2)}, u32[]{:S(2)}) collective-permute-start(bf16[24,12800]{1,0:T(8,128)(2,1)} %split.9), channel_id=1, source_target_pairs={{0,32},{32,0},{1,33},{33,1},{2,34},{34,2},{3,35},{35,3},{4,36},{36... | collective-permute-start | bytes 1843208 | tf_op jit(solution)/shard_map/ppermute | solution.py:22
  9.8 2.4 %reshape.147 = bf16[24,2,12800]{2,1,0:T(2,128)(2,1)} reshape(bf16[48,12800]{1,0:T(8,128)(2,1)} %param.9) | data formatting | bytes 2457600 | tf_op jit(solution)/shard_map/reshape | solution.py:129
  12.2 15.6 %all-to-all-start = ((bf16[24,2,12800]{2,1,0:T(2,128)(2,1)}), bf16[24,2,12800]{2,1,0:T(2,128)(2,1)}, u32[]{:S(2)}, u32[]{:S(2)}) async-start(bf16[24,2,12800]{2,1,0:T(2,128)(2,1)} %reshape.147), calls=%async_computation | async-start | bytes 2457600 | tf_op jit(solution)/shard_map/all_to_all | solution.py:130
  27.9 1.2 broadcast_select_fusion
  29.2 0.9 pad_maximum_fusion.11
  30.1 3.7 %collective-permute-start.11 = (bf16[4,12800]{1,0:T(4,128)(2,1)}, bf16[4,12800]{1,0:T(4,128)(2,1)}, u32[]{:S(2)}, u32[]{:S(2)}) collective-permute-start(bf16[4,12800]{1,0:T(4,128)(2,1)} %pad_maximum_fusion.11), channel_id=1, source_target_pairs={{0,64},{64,128},{128,192},{192,256},{256,320},{320,384},{384,448},... | collective-permute-start | bytes 307208 | tf_op jit(solution)/shard_map/ppermute | solution.py:27
  34.0 0.8 fusion.21
  34.9 0.8 pad_maximum_fusion.10
  35.6 4.3 %collective-permute-start.10 = (bf16[4,12800]{1,0:T(4,128)(2,1)}, bf16[4,12800]{1,0:T(4,128)(2,1)}, u32[]{:S(2)}, u32[]{:S(2)}) collective-permute-start(bf16[4,12800]{1,0:T(4,128)(2,1)} %pad_maximum_fusion.10), channel_id=1, source_target_pairs={{0,128},{64,192},{128,256},{192,320},{256,384},{320,448},{384,512}... | collective-permute-start | bytes 307208 | tf_op jit(solution)/shard_map/ppermute | solution.py:27
  39.9 0.7 pad_maximum_fusion.9
  40.6 6.4 %collective-permute-start.9 = (bf16[4,12800]{1,0:T(4,128)(2,1)}, bf16[4,12800]{1,0:T(4,128)(2,1)}, u32[]{:S(2)}, u32[]{:S(2)}) collective-permute-start(bf16[4,12800]{1,0:T(4,128)(2,1)} %pad_maximum_fusion.9), channel_id=1, source_target_pairs={{0,192},{64,256},{128,320},{192,384},{256,448},{320,512},{384,576}... | collective-permute-start | bytes 307208 | tf_op jit(solution)/shard_map/ppermute | solution.py:27
  47.4 0.8 pad_maximum_fusion.8
  48.1 3.1 %collective-permute-start.8 = (bf16[4,12800]{1,0:T(4,128)(2,1)}, bf16[4,12800]{1,0:T(4,128)(2,1)}, u32[]{:S(2)}, u32[]{:S(2)}) collective-permute-start(bf16[4,12800]{1,0:T(4,128)(2,1)} %pad_maximum_fusion.8), channel_id=1, source_target_pairs={{0,256},{64,320},{128,384},{192,448},{256,512},{320,576},{384,640}... | collective-permute-start | bytes 307208 | tf_op jit(solution)/shard_map/ppermute | solution.py:27
  51.2 0.8 pad_maximum_fusion.7
  52.0 5.1 %collective-permute-start.7 = (bf16[4,12800]{1,0:T(4,128)(2,1)}, bf16[4,12800]{1,0:T(4,128)(2,1)}, u32[]{:S(2)}, u32[]{:S(2)}) collective-permute-start(bf16[4,12800]{1,0:T(4,128)(2,1)} %pad_maximum_fusion.7), channel_id=1, source_target_pairs={{0,320},{64,384},{128,448},{192,512},{256,576},{320,640},{384,704}... | collective-permute-start | bytes 307208 | tf_op jit(solution)/shard_map/ppermute | solution.py:27
  57.1 0.8 pad_maximum_fusion.6
  59.4 0.8 pad_maximum_fusion.3
  60.9 14.3 %all-to-all-done = bf16[24,2,12800]{2,1,0:T(2,128)(2,1)} async-done(((bf16[24,2,12800]{2,1,0:T(2,128)(2,1)}), bf16[24,2,12800]{2,1,0:T(2,128)(2,1)}, u32[]{:S(2)}, u32[]{:S(2)}) %all-to-all-start) | async-done | bytes 1228832 | tf_op jit(solution)/shard_map/all_to_all | solution.py:130
  75.2 2.4 %reshape.148 = bf16[48,12800]{1,0:T(8,128)(2,1)} reshape(bf16[24,2,12800]{2,1,0:T(2,128)(2,1)} %all-to-all-done) | data formatting | bytes 2457600 | tf_op jit(solution)/shard_map/reshape | solution.py:137
  77.6 2.2 %multiply_reduce_fusion = (f32[12800]{0:T(1024)S(1)}, f32[32]{0:T(128)S(1)}, f32[32]{0:T(128)S(1)}, f32[12800]{0:T(1024)S(1)}, f32[32,12800]{1,0:T(8,128)S(1)}) fusion(f32[32,12800]{1,0:T(8,128)S(1)} %reshape.152, f32[32]{0:T(128)S(1)} %bitcast.23, f32[32]{0:T(128)S(1)} %bitcast.21, f32[12800]{0:T(1024)S(1)} %copy-done.2, bf16[48,12800]{1,0:T(8,128)(2,1)} %reshape.148, ...), kind=kOutput, calls=%fused_computation.3 | convolution fusion | flops 42983872 | bytes 4659840 | tf_op jit(solution)/shard_map/dot_general | solution.py:135
  80.5 10.2 %all-to-all-start.1 = ((f32[32,1,1024]{2,1,0:T(1,128)}), f32[32,1,1024]{2,1,0:T(1,128)S(1)}, u32[]{:S(2)}, u32[]{:S(2)}) async-start(f32[32,1,1024]{2,1,0:T(1,128)} %bitcast.5), calls=%async_computation.1 | async-start | bytes 262144 | tf_op jit(solution)/shard_map/all_to_all | solution.py:31
  90.7 3.4 %collective-permute-start.6 = (bf16[4,12800]{1,0:T(4,128)(2,1)}, bf16[4,12800]{1,0:T(4,128)(2,1)S(1)}, u32[]{:S(2)}, u32[]{:S(2)}) collective-permute-start(bf16[4,12800]{1,0:T(4,128)(2,1)} %pad_maximum_fusion.6), channel_id=1, source_target_pairs={{0,384},{64,448},{128,512},{192,576},{256,640},{320,704},{384,0},{... | collective-permute-start | bytes 307208 | tf_op jit(solution)/shard_map/ppermute | solution.py:27
  94.1 0.9 pad_maximum_fusion.1
  95.0 6.3 %collective-permute-start.5 = (bf16[4,12800]{1,0:T(4,128)(2,1)}, bf16[4,12800]{1,0:T(4,128)(2,1)}, u32[]{:S(2)}, u32[]{:S(2)}) collective-permute-start(bf16[4,12800]{1,0:T(4,128)(2,1)} %pad_maximum_fusion.5), channel_id=1, source_target_pairs={{0,448},{64,512},{128,576},{192,640},{256,704},{320,0},{384,64},{4... | collective-permute-start | bytes 307208 | tf_op jit(solution)/shard_map/ppermute | solution.py:27
  101.3 6.8 %collective-permute-start.4 = (bf16[4,12800]{1,0:T(4,128)(2,1)}, bf16[4,12800]{1,0:T(4,128)(2,1)}, u32[]{:S(2)}, u32[]{:S(2)}) collective-permute-start(bf16[4,12800]{1,0:T(4,128)(2,1)} %pad_maximum_fusion.4), channel_id=1, source_target_pairs={{0,512},{64,576},{128,640},{192,704},{256,0},{320,64},{384,128},{4... | collective-permute-start | bytes 307208 | tf_op jit(solution)/shard_map/ppermute | solution.py:27
  108.2 1.9 %collective-permute-start.3 = (bf16[4,12800]{1,0:T(4,128)(2,1)}, bf16[4,12800]{1,0:T(4,128)(2,1)}, u32[]{:S(2)}, u32[]{:S(2)}) collective-permute-start(bf16[4,12800]{1,0:T(4,128)(2,1)} %pad_maximum_fusion.3), channel_id=1, source_target_pairs={{0,576},{64,640},{128,704},{192,0},{256,64},{320,128},{384,192},{4... | collective-permute-start | bytes 307208 | tf_op jit(solution)/shard_map/ppermute | solution.py:27
  110.1 2.0 %collective-permute-done.7 = bf16[4,12800]{1,0:T(4,128)(2,1)} collective-permute-done((bf16[4,12800]{1,0:T(4,128)(2,1)}, bf16[4,12800]{1,0:T(4,128)(2,1)}, u32[]{:S(2)}, u32[]{:S(2)}) %collective-permute-start.7) | collective-permute-done | bytes 102432 | tf_op jit(solution)/shard_map/ppermute | solution.py:27
  112.1 1.9 %collective-permute-start.2 = (bf16[4,12800]{1,0:T(4,128)(2,1)}, bf16[4,12800]{1,0:T(4,128)(2,1)}, u32[]{:S(2)}, u32[]{:S(2)}) collective-permute-start(bf16[4,12800]{1,0:T(4,128)(2,1)} %pad_maximum_fusion.2), channel_id=1, source_target_pairs={{0,640},{64,704},{128,0},{192,64},{256,128},{320,192},{384,256},{4... | collective-permute-start | bytes 307208 | tf_op jit(solution)/shard_map/ppermute | solution.py:27
  114.1 3.6 %collective-permute-start.1 = (bf16[4,12800]{1,0:T(4,128)(2,1)S(1)}, bf16[4,12800]{1,0:T(4,128)(2,1)}, u32[]{:S(2)}, u32[]{:S(2)}) collective-permute-start(bf16[4,12800]{1,0:T(4,128)(2,1)S(1)} %pad_maximum_fusion.1), channel_id=1, source_target_pairs={{0,704},{64,0},{128,64},{192,128},{256,192},{320,256},{384,320},{4... | collective-permute-start | bytes 307208 | tf_op jit(solution)/shard_map/ppermute | solution.py:27
  117.7 1.0 slice.104
  118.7 1.6 slice.105
  120.3 3.3 %collective-permute-done.4 = bf16[4,12800]{1,0:T(4,128)(2,1)} collective-permute-done((bf16[4,12800]{1,0:T(4,128)(2,1)}, bf16[4,12800]{1,0:T(4,128)(2,1)}, u32[]{:S(2)}, u32[]{:S(2)}) %collective-permute-start.4) | collective-permute-done | bytes 102432 | tf_op jit(solution)/shard_map/ppermute | solution.py:27
  123.6 6.8 %collective-permute-done.3 = bf16[4,12800]{1,0:T(4,128)(2,1)} collective-permute-done((bf16[4,12800]{1,0:T(4,128)(2,1)}, bf16[4,12800]{1,0:T(4,128)(2,1)}, u32[]{:S(2)}, u32[]{:S(2)}) %collective-permute-start.3) | collective-permute-done | bytes 102432 | tf_op jit(solution)/shard_map/ppermute | solution.py:27
  130.4 4.7 %collective-permute-done.2 = bf16[4,12800]{1,0:T(4,128)(2,1)} collective-permute-done((bf16[4,12800]{1,0:T(4,128)(2,1)}, bf16[4,12800]{1,0:T(4,128)(2,1)}, u32[]{:S(2)}, u32[]{:S(2)}) %collective-permute-start.2) | collective-permute-done | bytes 102432 | tf_op jit(solution)/shard_map/ppermute | solution.py:27
  135.1 1.9 %collective-permute-done.1 = bf16[4,12800]{1,0:T(4,128)(2,1)} collective-permute-done((bf16[4,12800]{1,0:T(4,128)(2,1)S(1)}, bf16[4,12800]{1,0:T(4,128)(2,1)}, u32[]{:S(2)}, u32[]{:S(2)}) %collective-permute-start.1) | collective-permute-done | bytes 102432 | tf_op jit(solution)/shard_map/ppermute | solution.py:27
  137.0 9.8 %concatenate.54 = bf16[48,12800]{1,0:T(8,128)(2,1)} concatenate(bf16[2,12800]{1,0:T(2,128)(2,1)S(1)} %slice.104, bf16[2,12800]{1,0:T(2,128)(2,1)} %slice.105, bf16[4,12800]{1,0:T(4,128)(2,1)} %collective-permute-done.1, bf16[4,12800]{1,0:T(4,128)(2,1)} %collective-permute-done.2, bf16[4,12800]{1,0:T(4,128)(2,1)} %collective-permute-done.3, ...), dimensions={0} | concatenate | bytes 2457600 | tf_op jit(solution)/shard_map/concatenate | solution.py:80
  147.6 5.2 %all-to-all-start.2 = ((f32[24,1,1024]{2,1,0:T(1,128)}), f32[24,1,1024]{2,1,0:T(1,128)S(1)}, u32[]{:S(2)}, u32[]{:S(2)}) async-start(f32[24,1,1024]{2,1,0:T(1,128)} %broadcast_in_dim.7), calls=%async_computation.2 | async-start | bytes 196608 | tf_op jit(solution)/shard_map/all_to_all | solution.py:31
  152.8 2.8 %convolution_convert_fusion = bf16[48,12800]{1,0:T(8,128)(2,1)} fusion(bf16[48,12800]{1,0:T(8,128)(2,1)} %concatenate.54, s32[48]{0:T(128)S(1)} %fusion.11), kind=kOutput, calls=%fused_computation | convolution fusion | flops 59599104 | bytes 2457792 | tf_op jit(solution)/shard_map/dot_general | solution.py:54
  155.7 8.6 %all-to-all-done.2 = f32[24,1,1024]{2,1,0:T(1,128)S(1)} async-done(((f32[24,1,1024]{2,1,0:T(1,128)}), f32[24,1,1024]{2,1,0:T(1,128)S(1)}, u32[]{:S(2)}, u32[]{:S(2)}) %all-to-all-start.2) | async-done | bytes 98336 | tf_op jit(solution)/shard_map/all_to_all | solution.py:31
  165.1 9.8 %all-to-all-start.3 = ((f32[32,1,1024]{2,1,0:T(1,128)}), f32[32,1,1024]{2,1,0:T(1,128)S(1)}, u32[]{:S(2)}, u32[]{:S(2)}) async-start(f32[32,1,1024]{2,1,0:T(1,128)} %broadcast_in_dim.8), calls=%async_computation.3 | async-start | bytes 262144 | tf_op jit(solution)/shard_map/all_to_all | solution.py:31
  174.9 1.4 multiply_convert_fusion
  176.2 2.3 %reshape.149 = bf16[2,16,2,2,3200]{4,3,2,1,0:T(2,128)(2,1)S(1)} reshape(bf16[32,12800]{1,0:T(8,128)(2,1)} %multiply_convert_fusion) | data formatting | bytes 1638400 | tf_op jit(solution)/shard_map/reshape | solution.py:93
  179.1 1.2 reshape.150
  180.3 3.5 %all-to-all-done.3 = f32[32,1,1024]{2,1,0:T(1,128)S(1)} async-done(((f32[32,1,1024]{2,1,0:T(1,128)}), f32[32,1,1024]{2,1,0:T(1,128)S(1)}, u32[]{:S(2)}, u32[]{:S(2)}) %all-to-all-start.3) | async-done | bytes 131104 | tf_op jit(solution)/shard_map/all_to_all | solution.py:31
  (53 shorter events, 8.3 us)
Async XLA Ops:
  4.6 1.3 copy-start.5
  4.6 1.9 %copy-start.2 = (f32[12800]{0:T(1024)S(1)}, f32[12800]{0:T(1024)}, u32[]{:S(2)}) copy-start(f32[12800]{0:T(1024)} %param.7) | copy-start | bytes 153604
  4.6 1.9 %copy-start.4 = (f32[12800]{0:T(1024)S(1)}, f32[12800]{0:T(1024)}, u32[]{:S(2)}) copy-start(f32[12800]{0:T(1024)} %param.8) | copy-start | bytes 153604
  7.9 20.0 %collective-permute-start = (bf16[24,12800]{1,0:T(8,128)(2,1)}, bf16[24,12800]{1,0:T(8,128)(2,1)}, u32[]{:S(2)}, u32[]{:S(2)}) collective-permute-start(bf16[24,12800]{1,0:T(8,128)(2,1)} %split.9), channel_id=1, source_target_pairs={{0,32},{32,0},{1,33},{33,1},{2,34},{34,2},{3,35},{35,3},{4,36},{36... | collective-permute-start | bytes 1843208 | tf_op jit(solution)/shard_map/ppermute | solution.py:22
  12.2 63.0 %all-to-all-start = ((bf16[24,2,12800]{2,1,0:T(2,128)(2,1)}), bf16[24,2,12800]{2,1,0:T(2,128)(2,1)}, u32[]{:S(2)}, u32[]{:S(2)}) async-start(bf16[24,2,12800]{2,1,0:T(2,128)(2,1)} %reshape.147), calls=%async_computation | async-start | bytes 2457600 | tf_op jit(solution)/shard_map/all_to_all | solution.py:130
  29.1 22.9 %copy-start = (bf16[24,12800]{1,0:T(8,128)(2,1)}, bf16[24,12800]{1,0:T(8,128)(2,1)S(1)}, u32[]{:S(2)}) copy-start(bf16[24,12800]{1,0:T(8,128)(2,1)S(1)} %get-tuple-element.19) | copy-start | bytes 1843204
  29.1 22.9 %copy-start.1 = (bf16[24,12800]{1,0:T(8,128)(2,1)}, bf16[24,12800]{1,0:T(8,128)(2,1)S(1)}, u32[]{:S(2)}) copy-start(bf16[24,12800]{1,0:T(8,128)(2,1)S(1)} %get-tuple-element.18) | copy-start | bytes 1843204
  30.1 60.6 %collective-permute-start.11 = (bf16[4,12800]{1,0:T(4,128)(2,1)}, bf16[4,12800]{1,0:T(4,128)(2,1)}, u32[]{:S(2)}, u32[]{:S(2)}) collective-permute-start(bf16[4,12800]{1,0:T(4,128)(2,1)} %pad_maximum_fusion.11), channel_id=1, source_target_pairs={{0,64},{64,128},{128,192},{192,256},{256,320},{320,384},{384,448},... | collective-permute-start | bytes 307208 | tf_op jit(solution)/shard_map/ppermute | solution.py:27
  35.6 59.4 %collective-permute-start.10 = (bf16[4,12800]{1,0:T(4,128)(2,1)}, bf16[4,12800]{1,0:T(4,128)(2,1)}, u32[]{:S(2)}, u32[]{:S(2)}) collective-permute-start(bf16[4,12800]{1,0:T(4,128)(2,1)} %pad_maximum_fusion.10), channel_id=1, source_target_pairs={{0,128},{64,192},{128,256},{192,320},{256,384},{320,448},{384,512}... | collective-permute-start | bytes 307208 | tf_op jit(solution)/shard_map/ppermute | solution.py:27
  40.6 60.7 %collective-permute-start.9 = (bf16[4,12800]{1,0:T(4,128)(2,1)}, bf16[4,12800]{1,0:T(4,128)(2,1)}, u32[]{:S(2)}, u32[]{:S(2)}) collective-permute-start(bf16[4,12800]{1,0:T(4,128)(2,1)} %pad_maximum_fusion.9), channel_id=1, source_target_pairs={{0,192},{64,256},{128,320},{192,384},{256,448},{320,512},{384,576}... | collective-permute-start | bytes 307208 | tf_op jit(solution)/shard_map/ppermute | solution.py:27
  48.1 60.0 %collective-permute-start.8 = (bf16[4,12800]{1,0:T(4,128)(2,1)}, bf16[4,12800]{1,0:T(4,128)(2,1)}, u32[]{:S(2)}, u32[]{:S(2)}) collective-permute-start(bf16[4,12800]{1,0:T(4,128)(2,1)} %pad_maximum_fusion.8), channel_id=1, source_target_pairs={{0,256},{64,320},{128,384},{192,448},{256,512},{320,576},{384,640}... | collective-permute-start | bytes 307208 | tf_op jit(solution)/shard_map/ppermute | solution.py:27
  52.0 60.1 %collective-permute-start.7 = (bf16[4,12800]{1,0:T(4,128)(2,1)}, bf16[4,12800]{1,0:T(4,128)(2,1)}, u32[]{:S(2)}, u32[]{:S(2)}) collective-permute-start(bf16[4,12800]{1,0:T(4,128)(2,1)} %pad_maximum_fusion.7), channel_id=1, source_target_pairs={{0,320},{64,384},{128,448},{192,512},{256,576},{320,640},{384,704}... | collective-permute-start | bytes 307208 | tf_op jit(solution)/shard_map/ppermute | solution.py:27
  80.5 66.3 %all-to-all-start.1 = ((f32[32,1,1024]{2,1,0:T(1,128)}), f32[32,1,1024]{2,1,0:T(1,128)S(1)}, u32[]{:S(2)}, u32[]{:S(2)}) async-start(f32[32,1,1024]{2,1,0:T(1,128)} %bitcast.5), calls=%async_computation.1 | async-start | bytes 262144 | tf_op jit(solution)/shard_map/all_to_all | solution.py:31
  90.7 23.3 %collective-permute-start.6 = (bf16[4,12800]{1,0:T(4,128)(2,1)}, bf16[4,12800]{1,0:T(4,128)(2,1)S(1)}, u32[]{:S(2)}, u32[]{:S(2)}) collective-permute-start(bf16[4,12800]{1,0:T(4,128)(2,1)} %pad_maximum_fusion.6), channel_id=1, source_target_pairs={{0,384},{64,448},{128,512},{192,576},{256,640},{320,704},{384,0},{... | collective-permute-start | bytes 307208 | tf_op jit(solution)/shard_map/ppermute | solution.py:27
  95.0 25.2 %collective-permute-start.5 = (bf16[4,12800]{1,0:T(4,128)(2,1)}, bf16[4,12800]{1,0:T(4,128)(2,1)}, u32[]{:S(2)}, u32[]{:S(2)}) collective-permute-start(bf16[4,12800]{1,0:T(4,128)(2,1)} %pad_maximum_fusion.5), channel_id=1, source_target_pairs={{0,448},{64,512},{128,576},{192,640},{256,704},{320,0},{384,64},{4... | collective-permute-start | bytes 307208 | tf_op jit(solution)/shard_map/ppermute | solution.py:27
  101.3 22.3 %collective-permute-start.4 = (bf16[4,12800]{1,0:T(4,128)(2,1)}, bf16[4,12800]{1,0:T(4,128)(2,1)}, u32[]{:S(2)}, u32[]{:S(2)}) collective-permute-start(bf16[4,12800]{1,0:T(4,128)(2,1)} %pad_maximum_fusion.4), channel_id=1, source_target_pairs={{0,512},{64,576},{128,640},{192,704},{256,0},{320,64},{384,128},{4... | collective-permute-start | bytes 307208 | tf_op jit(solution)/shard_map/ppermute | solution.py:27
  108.2 22.2 %collective-permute-start.3 = (bf16[4,12800]{1,0:T(4,128)(2,1)}, bf16[4,12800]{1,0:T(4,128)(2,1)}, u32[]{:S(2)}, u32[]{:S(2)}) collective-permute-start(bf16[4,12800]{1,0:T(4,128)(2,1)} %pad_maximum_fusion.3), channel_id=1, source_target_pairs={{0,576},{64,640},{128,704},{192,0},{256,64},{320,128},{384,192},{4... | collective-permute-start | bytes 307208 | tf_op jit(solution)/shard_map/ppermute | solution.py:27
  112.1 23.0 %collective-permute-start.2 = (bf16[4,12800]{1,0:T(4,128)(2,1)}, bf16[4,12800]{1,0:T(4,128)(2,1)}, u32[]{:S(2)}, u32[]{:S(2)}) collective-permute-start(bf16[4,12800]{1,0:T(4,128)(2,1)} %pad_maximum_fusion.2), channel_id=1, source_target_pairs={{0,640},{64,704},{128,0},{192,64},{256,128},{320,192},{384,256},{4... | collective-permute-start | bytes 307208 | tf_op jit(solution)/shard_map/ppermute | solution.py:27
  114.0 3.7 %copy-start.3 = (bf16[4,12800]{1,0:T(4,128)(2,1)}, bf16[4,12800]{1,0:T(4,128)(2,1)S(1)}, u32[]{:S(2)}) copy-start(bf16[4,12800]{1,0:T(4,128)(2,1)S(1)} %collective-permute-done.6) | copy-start | bytes 307204
  114.1 22.9 %collective-permute-start.1 = (bf16[4,12800]{1,0:T(4,128)(2,1)S(1)}, bf16[4,12800]{1,0:T(4,128)(2,1)}, u32[]{:S(2)}, u32[]{:S(2)}) collective-permute-start(bf16[4,12800]{1,0:T(4,128)(2,1)S(1)} %pad_maximum_fusion.1), channel_id=1, source_target_pairs={{0,704},{64,0},{128,64},{192,128},{256,192},{320,256},{384,320},{4... | collective-permute-start | bytes 307208 | tf_op jit(solution)/shard_map/ppermute | solution.py:27
  147.6 16.7 %all-to-all-start.2 = ((f32[24,1,1024]{2,1,0:T(1,128)}), f32[24,1,1024]{2,1,0:T(1,128)S(1)}, u32[]{:S(2)}, u32[]{:S(2)}) async-start(f32[24,1,1024]{2,1,0:T(1,128)} %broadcast_in_dim.7), calls=%async_computation.2 | async-start | bytes 196608 | tf_op jit(solution)/shard_map/all_to_all | solution.py:31
  165.1 18.7 %all-to-all-start.3 = ((f32[32,1,1024]{2,1,0:T(1,128)}), f32[32,1,1024]{2,1,0:T(1,128)S(1)}, u32[]{:S(2)}, u32[]{:S(2)}) async-start(f32[32,1,1024]{2,1,0:T(1,128)} %broadcast_in_dim.8), calls=%async_computation.3 | async-start | bytes 262144 | tf_op jit(solution)/shard_map/all_to_all | solution.py:31

commit v5 on v4

--- a/solution.py
+++ b/solution.py
@@ -70,17 +70,21 @@
         cut = slice(by * capacity, (by + 1) * capacity)
         return jnp.concatenate([half[cut] for half in rows])
 
-    came = {0: block(0)}
+    came = {}
+    tops = [half[:8] for half in rows]
     plan = (FAR, MID, NEAR)
     for group in plan:
         rows = lax.optimization_barrier(rows)
         for by in group:
             piece = block(by)
             came[by] = shifted(piece, "z", by)
-    joined = jnp.concatenate([came[-j % deep] for j in range(deep)])
+    joined = jnp.concatenate([*tops, *(came[-j % deep] for j in range(1, deep))])
     slot = jnp.arange(deep * wide, dtype=jnp.int32)
-    source = (slot // wide - z) % deep * wide + slot % wide
-    return picked(one_hot_rows(source, slot), joined)
+    ahead, within = (slot // wide - z) % deep, slot % wide
+    here = within // capacity * 8 + within % capacity
+    source = jnp.where(ahead == 0, here, 16 + (ahead - 1) * wide + within)
+    kept = jnp.arange(joined.shape[0], dtype=jnp.int32)
+    return picked(one_hot_rows(source, kept), joined)
 
 
 def shuffle_tokens(patches):

time: 187 us -> 184 us (0.984)
  local copies, waits for them, and re-layouts: 29 us -> 24.2 us
  waiting for transfers between devices: 45.1 us -> 47.8 us
    all_to_all x3, waiting for transfers between devices: 12.1 us -> 14.8 us  [exchanged(): return lax.all_to_all(value, axis, split_axis=0, concat_axis=0, tiled=True)]
    slice x0 -> x2, local copies, waits for them, and re-layouts: none -> 2.32 us  [delivered(): tops = [half[:8] for half in rows]]
    reshape x1, local copies, waits for them, and re-layouts: 2.33 us -> 0.19 us  [unshuffle_tokens(): grouped = tokens.reshape(height // 2, across // 2, 2, 2, channels)]
    concatenate x1, local copies, waits for them, and re-layouts: 9.79 us -> 7.74 us  [delivered(): jnp.concatenate([*tops, *(came[-j % deep] for j in range(1, deep))])]
    slice x8 -> x6, local copies, waits for them, and re-layouts: 4.09 us -> 2.16 us  [block(): return jnp.concatenate([half[cut] for half in rows])]
  transfers between devices with their start and end apart: 16 -> 16, of which waited for: 8 -> 8; matrix products, arithmetic and copies ran while one was open for 22% -> 19% of each run, Pallas kernels for 0% -> 0%
where the time goes in v5:
time: 184 us; the launch traced here: 182 us
  starting transfers between devices  88.6 us (48%)
  waiting for transfers between devices  47.8 us (26%)
  local copies, waits for them, and re-layouts  24.2 us (13%)
  other arithmetic  15.8 us (9%)
  matrix products  4.19 us (2%)
    ppermute x11, starting transfers between devices, shifted(): lax.ppermute(value, axis, [(i, (i + by) % size) for i in range(size)])  45.6 us
    all_to_all x3, starting transfers between devices, exchanged(): return lax.all_to_all(value, axis, split_axis=0, concat_axis=0, tiled=True)  25.5 us
    ppermute x11, waiting for transfers between devices, shifted(): lax.ppermute(value, axis, [(i, (i + by) % size) for i in range(size)])  19.1 us
    all_to_all x1, starting transfers between devices, steps(): lax.all_to_all(slots, ENC, split_axis=0, concat_axis=0, tiled=True)  15.6 us
    all_to_all x3, waiting for transfers between devices, exchanged(): return lax.all_to_all(value, axis, split_axis=0, concat_axis=0, tiled=True)  14.8 us
    all_to_all x1, waiting for transfers between devices, steps(): lax.all_to_all(slots, ENC, split_axis=0, concat_axis=0, tiled=True)  13.9 us
    concatenate x11, other arithmetic, block(): return jnp.concatenate([half[cut] for half in rows])  8.42 us
    concatenate x1, local copies, waits for them, and re-layouts, delivered(): jnp.concatenate([*tops, *(came[-j % deep] for j in range(1, deep))])  7.74 us
  transfers between devices with their start and end apart: 16, of which 8 were waited for; matrix products, arithmetic and copies ran while one was open for 19% of the time, Pallas kernels for 0%

profile of v5, /device:TPU:6, one launch (start us, length us, event | category | flops | bytes accessed | tf_op | source)
XLA Modules:
  0.0 181.6 jit_solution(12734243150460101526)
XLA Ops:
  0.6 2.2 %reshape.186 = f32[2,2,16,2,3200]{4,3,2,1,0:T(2,128)S(1)} reshape(bf16[4,32,3200]{2,1,0:T(8,128)(2,1)} %param.5) | data formatting | bytes 2457600 | tf_op jit(solution)/shard_map/convert_element_type | solution.py:103
  3.4 1.0 multiply_reduce_fusion.2
  4.6 1.3 reshape.184
  7.0 1.9 %collective-permute-start = (bf16[24,12800]{1,0:T(8,128)(2,1)S(1)}, bf16[24,12800]{1,0:T(8,128)(2,1)}, u32[]{:S(2)}, u32[]{:S(2)}) collective-permute-start(bf16[24,12800]{1,0:T(8,128)(2,1)S(1)} %split.9), channel_id=1, source_target_pairs={{0,32},{32,0},{1,33},{33,1},{2,34},{34,2},{3,35},{35,3},{4,36},{36... | collective-permute-start | bytes 1843208 | tf_op jit(solution)/shard_map/ppermute | solution.py:22
  9.0 2.4 %reshape.179 = bf16[24,2,12800]{2,1,0:T(2,128)(2,1)} reshape(bf16[48,12800]{1,0:T(8,128)(2,1)} %param.9) | data formatting | bytes 2457600 | tf_op jit(solution)/shard_map/reshape | solution.py:133
  11.4 15.6 %all-to-all-start = ((bf16[24,2,12800]{2,1,0:T(2,128)(2,1)}), bf16[24,2,12800]{2,1,0:T(2,128)(2,1)}, u32[]{:S(2)}, u32[]{:S(2)}) async-start(bf16[24,2,12800]{2,1,0:T(2,128)(2,1)} %reshape.179), calls=%async_computation | async-start | bytes 2457600 | tf_op jit(solution)/shard_map/all_to_all | solution.py:134
  27.1 1.2 broadcast_select_fusion
  28.4 0.8 pad_maximum_fusion.11
  29.1 3.7 %collective-permute-start.11 = (bf16[4,12800]{1,0:T(4,128)(2,1)}, bf16[4,12800]{1,0:T(4,128)(2,1)}, u32[]{:S(2)}, u32[]{:S(2)}) collective-permute-start(bf16[4,12800]{1,0:T(4,128)(2,1)} %pad_maximum_fusion.11), channel_id=1, source_target_pairs={{0,64},{64,128},{128,192},{192,256},{256,320},{320,384},{384,448},... | collective-permute-start | bytes 307208 | tf_op jit(solution)/shard_map/ppermute | solution.py:27
  32.8 0.8 fusion.19
  33.7 0.8 fusion.20
  34.5 0.8 pad_maximum_fusion.10
  35.3 4.3 %collective-permute-start.10 = (bf16[4,12800]{1,0:T(4,128)(2,1)}, bf16[4,12800]{1,0:T(4,128)(2,1)}, u32[]{:S(2)}, u32[]{:S(2)}) collective-permute-start(bf16[4,12800]{1,0:T(4,128)(2,1)} %pad_maximum_fusion.10), channel_id=1, source_target_pairs={{0,128},{64,192},{128,256},{192,320},{256,384},{320,448},{384,512}... | collective-permute-start | bytes 307208 | tf_op jit(solution)/shard_map/ppermute | solution.py:27
  39.6 0.7 pad_maximum_fusion.9
  40.3 6.4 %collective-permute-start.9 = (bf16[4,12800]{1,0:T(4,128)(2,1)}, bf16[4,12800]{1,0:T(4,128)(2,1)}, u32[]{:S(2)}, u32[]{:S(2)}) collective-permute-start(bf16[4,12800]{1,0:T(4,128)(2,1)} %pad_maximum_fusion.9), channel_id=1, source_target_pairs={{0,192},{64,256},{128,320},{192,384},{256,448},{320,512},{384,576}... | collective-permute-start | bytes 307208 | tf_op jit(solution)/shard_map/ppermute | solution.py:27
  47.1 0.8 pad_maximum_fusion.8
  47.8 3.1 %collective-permute-start.8 = (bf16[4,12800]{1,0:T(4,128)(2,1)}, bf16[4,12800]{1,0:T(4,128)(2,1)}, u32[]{:S(2)}, u32[]{:S(2)}) collective-permute-start(bf16[4,12800]{1,0:T(4,128)(2,1)} %pad_maximum_fusion.8), channel_id=1, source_target_pairs={{0,256},{64,320},{128,384},{192,448},{256,512},{320,576},{384,640}... | collective-permute-start | bytes 307208 | tf_op jit(solution)/shard_map/ppermute | solution.py:27
  51.6 5.1 %collective-permute-start.7 = (bf16[4,12800]{1,0:T(4,128)(2,1)}, bf16[4,12800]{1,0:T(4,128)(2,1)}, u32[]{:S(2)}, u32[]{:S(2)}) collective-permute-start(bf16[4,12800]{1,0:T(4,128)(2,1)} %pad_maximum_fusion.7), channel_id=1, source_target_pairs={{0,320},{64,384},{128,448},{192,512},{256,576},{320,640},{384,704}... | collective-permute-start | bytes 307208 | tf_op jit(solution)/shard_map/ppermute | solution.py:27
  56.8 0.7 pad_maximum_fusion.6
  57.5 0.7 pad_maximum_fusion.5
  58.3 0.8 pad_maximum_fusion.4
  59.8 0.7 pad_maximum_fusion.2
  60.5 13.9 %all-to-all-done = bf16[24,2,12800]{2,1,0:T(2,128)(2,1)} async-done(((bf16[24,2,12800]{2,1,0:T(2,128)(2,1)}), bf16[24,2,12800]{2,1,0:T(2,128)(2,1)}, u32[]{:S(2)}, u32[]{:S(2)}) %all-to-all-start) | async-done | bytes 1228832 | tf_op jit(solution)/shard_map/all_to_all | solution.py:134
  74.4 1.6 reshape.180
  76.0 2.1 %multiply_reduce_fusion = (f32[12800]{0:T(1024)S(1)}, f32[32]{0:T(128)S(1)}, f32[32]{0:T(128)S(1)}, f32[12800]{0:T(1024)S(1)}, f32[32,12800]{1,0:T(8,128)}) fusion(f32[32,12800]{1,0:T(8,128)S(1)} %reshape.184, f32[32]{0:T(128)S(1)} %bitcast.23, f32[32]{0:T(128)S(1)} %bitcast.21, f32[12800]{0:T(1024)S(1)} %copy-done.1, bf16[48,12800]{1,0:T(8,128)(2,1)S(1)} %reshape.180, ...), kind=kOutput, calls=%fused_computation.3 | convolution fusion | flops 42983872 | bytes 4659840 | tf_op jit(solution)/shard_map/dot_general | solution.py:139
  78.7 10.2 %all-to-all-start.1 = ((f32[32,1,1024]{2,1,0:T(1,128)}), f32[32,1,1024]{2,1,0:T(1,128)}, u32[]{:S(2)}, u32[]{:S(2)}) async-start(f32[32,1,1024]{2,1,0:T(1,128)} %bitcast.5), calls=%async_computation.1 | async-start | bytes 262144 | tf_op jit(solution)/shard_map/all_to_all | solution.py:31
  89.0 3.4 %collective-permute-start.6 = (bf16[4,12800]{1,0:T(4,128)(2,1)}, bf16[4,12800]{1,0:T(4,128)(2,1)S(1)}, u32[]{:S(2)}, u32[]{:S(2)}) collective-permute-start(bf16[4,12800]{1,0:T(4,128)(2,1)} %pad_maximum_fusion.6), channel_id=1, source_target_pairs={{0,384},{64,448},{128,512},{192,576},{256,640},{320,704},{384,0},{... | collective-permute-start | bytes 307208 | tf_op jit(solution)/shard_map/ppermute | solution.py:27
  92.4 0.9 pad_maximum_fusion.1
  93.4 6.3 %collective-permute-start.5 = (bf16[4,12800]{1,0:T(4,128)(2,1)}, bf16[4,12800]{1,0:T(4,128)(2,1)S(1)}, u32[]{:S(2)}, u32[]{:S(2)}) collective-permute-start(bf16[4,12800]{1,0:T(4,128)(2,1)} %pad_maximum_fusion.5), channel_id=1, source_target_pairs={{0,448},{64,512},{128,576},{192,640},{256,704},{320,0},{384,64},{4... | collective-permute-start | bytes 307208 | tf_op jit(solution)/shard_map/ppermute | solution.py:27
  99.7 6.8 %collective-permute-start.4 = (bf16[4,12800]{1,0:T(4,128)(2,1)}, bf16[4,12800]{1,0:T(4,128)(2,1)S(1)}, u32[]{:S(2)}, u32[]{:S(2)}) collective-permute-start(bf16[4,12800]{1,0:T(4,128)(2,1)} %pad_maximum_fusion.4), channel_id=1, source_target_pairs={{0,512},{64,576},{128,640},{192,704},{256,0},{320,64},{384,128},{4... | collective-permute-start | bytes 307208 | tf_op jit(solution)/shard_map/ppermute | solution.py:27
  106.5 1.9 %collective-permute-start.3 = (bf16[4,12800]{1,0:T(4,128)(2,1)}, bf16[4,12800]{1,0:T(4,128)(2,1)S(1)}, u32[]{:S(2)}, u32[]{:S(2)}) collective-permute-start(bf16[4,12800]{1,0:T(4,128)(2,1)} %pad_maximum_fusion.3), channel_id=1, source_target_pairs={{0,576},{64,640},{128,704},{192,0},{256,64},{320,128},{384,192},{4... | collective-permute-start | bytes 307208 | tf_op jit(solution)/shard_map/ppermute | solution.py:27
  108.4 2.9 %collective-permute-done.7 = bf16[4,12800]{1,0:T(4,128)(2,1)} collective-permute-done((bf16[4,12800]{1,0:T(4,128)(2,1)}, bf16[4,12800]{1,0:T(4,128)(2,1)}, u32[]{:S(2)}, u32[]{:S(2)}) %collective-permute-start.7) | collective-permute-done | bytes 102432 | tf_op jit(solution)/shard_map/ppermute | solution.py:27
  111.3 1.9 %collective-permute-start.2 = (bf16[4,12800]{1,0:T(4,128)(2,1)}, bf16[4,12800]{1,0:T(4,128)(2,1)S(1)}, u32[]{:S(2)}, u32[]{:S(2)}) collective-permute-start(bf16[4,12800]{1,0:T(4,128)(2,1)} %pad_maximum_fusion.2), channel_id=1, source_target_pairs={{0,640},{64,704},{128,0},{192,64},{256,128},{320,192},{384,256},{4... | collective-permute-start | bytes 307208 | tf_op jit(solution)/shard_map/ppermute | solution.py:27
  113.2 2.8 %collective-permute-start.1 = (bf16[4,12800]{1,0:T(4,128)(2,1)S(1)}, bf16[4,12800]{1,0:T(4,128)(2,1)}, u32[]{:S(2)}, u32[]{:S(2)}) collective-permute-start(bf16[4,12800]{1,0:T(4,128)(2,1)S(1)} %pad_maximum_fusion.1), channel_id=1, source_target_pairs={{0,704},{64,0},{128,64},{192,128},{256,192},{320,256},{384,320},{4... | collective-permute-start | bytes 307208 | tf_op jit(solution)/shard_map/ppermute | solution.py:27
  116.0 1.6 slice.104
  118.4 3.4 %collective-permute-done.4 = bf16[4,12800]{1,0:T(4,128)(2,1)S(1)} collective-permute-done((bf16[4,12800]{1,0:T(4,128)(2,1)}, bf16[4,12800]{1,0:T(4,128)(2,1)S(1)}, u32[]{:S(2)}, u32[]{:S(2)}) %collective-permute-start.4) | collective-permute-done | bytes 102432 | tf_op jit(solution)/shard_map/ppermute | solution.py:27
  121.8 6.8 %collective-permute-done.3 = bf16[4,12800]{1,0:T(4,128)(2,1)S(1)} collective-permute-done((bf16[4,12800]{1,0:T(4,128)(2,1)}, bf16[4,12800]{1,0:T(4,128)(2,1)S(1)}, u32[]{:S(2)}, u32[]{:S(2)}) %collective-permute-start.3) | collective-permute-done | bytes 102432 | tf_op jit(solution)/shard_map/ppermute | solution.py:27
  128.6 4.7 %collective-permute-done.2 = bf16[4,12800]{1,0:T(4,128)(2,1)S(1)} collective-permute-done((bf16[4,12800]{1,0:T(4,128)(2,1)}, bf16[4,12800]{1,0:T(4,128)(2,1)S(1)}, u32[]{:S(2)}, u32[]{:S(2)}) %collective-permute-start.2) | collective-permute-done | bytes 102432 | tf_op jit(solution)/shard_map/ppermute | solution.py:27
  134.0 1.3 collective-permute-done.1
  135.3 7.7 %concatenate.54 = bf16[60,12800]{1,0:T(8,128)(2,1)S(1)} concatenate(bf16[8,12800]{1,0:T(8,128)(2,1)} %slice.104, bf16[8,12800]{1,0:T(8,128)(2,1)} %slice.105, bf16[4,12800]{1,0:T(4,128)(2,1)} %collective-permute-done.1, bf16[4,12800]{1,0:T(4,128)(2,1)} %copy-done.6, bf16[4,12800]{1,0:T(4,128)(2,1)} %copy-done.5, bf16[4,12800]{1,0:T(4,128)(2,1)} %copy-done.4, ...), dimensions={0} | concatenate | bytes 3072000 | tf_op jit(solution)/shard_map/concatenate | solution.py:81
  143.0 1.0 reduce_sum.88
  144.7 5.4 %all-to-all-start.2 = ((f32[24,1,1024]{2,1,0:T(1,128)}), f32[24,1,1024]{2,1,0:T(1,128)S(1)}, u32[]{:S(2)}, u32[]{:S(2)}) async-start(f32[24,1,1024]{2,1,0:T(1,128)} %broadcast_in_dim.7), calls=%async_computation.2 | async-start | bytes 196608 | tf_op jit(solution)/shard_map/all_to_all | solution.py:31
  150.2 1.6 convolution_convert_fusion
  151.7 9.7 %all-to-all-done.2 = f32[24,1,1024]{2,1,0:T(1,128)S(1)} async-done(((f32[24,1,1024]{2,1,0:T(1,128)}), f32[24,1,1024]{2,1,0:T(1,128)S(1)}, u32[]{:S(2)}, u32[]{:S(2)}) %all-to-all-start.2) | async-done | bytes 98336 | tf_op jit(solution)/shard_map/all_to_all | solution.py:31
  162.3 9.8 %all-to-all-start.3 = ((f32[32,1,1024]{2,1,0:T(1,128)}), f32[32,1,1024]{2,1,0:T(1,128)S(1)}, u32[]{:S(2)}, u32[]{:S(2)}) async-start(f32[32,1,1024]{2,1,0:T(1,128)} %broadcast_in_dim.8), calls=%async_computation.3 | async-start | bytes 262144 | tf_op jit(solution)/shard_map/all_to_all | solution.py:31
  172.0 1.9 %multiply_convert_fusion = bf16[32,12800]{1,0:T(8,128)(2,1)S(1)} fusion(f32[32,12800]{1,0:T(8,128)} %get-tuple-element.52, f32[32,12800]{1,0:T(8,128)S(1)} %reshape.184, f32[32]{0:T(128)S(1)} %get-tuple-element.55, f32[32]{0:T(128)S(1)} %bitcast.24, f32[32]{0:T(128)S(1)} %get-tuple-element.56, f32[32]{0:T(128)S(1)} %bitcast.22, f32[12800]{0:T(1024)S(1)} %copy-done.1), kind=kLoop, calls=%fused_computation.4 | loop fusion | flops 3276800 | bytes 4147712 | tf_op jit(solution)/shard_map/convert_element_type | solution.py:115
  174.7 1.2 reshape.182
  175.9 5.0 %all-to-all-done.3 = f32[32,1,1024]{2,1,0:T(1,128)S(1)} async-done(((f32[32,1,1024]{2,1,0:T(1,128)}), f32[32,1,1024]{2,1,0:T(1,128)S(1)}, u32[]{:S(2)}, u32[]{:S(2)}) %all-to-all-start.3) | async-done | bytes 131104 | tf_op jit(solution)/shard_map/all_to_all | solution.py:31
  (59 shorter events, 8.8 us)
Async XLA Ops:
  4.6 1.3 copy-start.8
  4.6 1.9 %copy-start.1 = (f32[12800]{0:T(1024)S(1)}, f32[12800]{0:T(1024)}, u32[]{:S(2)}) copy-start(f32[12800]{0:T(1024)} %param.7) | copy-start | bytes 153604
  4.6 1.9 %copy-start.7 = (f32[12800]{0:T(1024)S(1)}, f32[12800]{0:T(1024)}, u32[]{:S(2)}) copy-start(f32[12800]{0:T(1024)} %param.8) | copy-start | bytes 153604
  7.0 20.0 %collective-permute-start = (bf16[24,12800]{1,0:T(8,128)(2,1)S(1)}, bf16[24,12800]{1,0:T(8,128)(2,1)}, u32[]{:S(2)}, u32[]{:S(2)}) collective-permute-start(bf16[24,12800]{1,0:T(8,128)(2,1)S(1)} %split.9), channel_id=1, source_target_pairs={{0,32},{32,0},{1,33},{33,1},{2,34},{34,2},{3,35},{35,3},{4,36},{36... | collective-permute-start | bytes 1843208 | tf_op jit(solution)/shard_map/ppermute | solution.py:22
  11.4 63.0 %all-to-all-start = ((bf16[24,2,12800]{2,1,0:T(2,128)(2,1)}), bf16[24,2,12800]{2,1,0:T(2,128)(2,1)}, u32[]{:S(2)}, u32[]{:S(2)}) async-start(bf16[24,2,12800]{2,1,0:T(2,128)(2,1)} %reshape.179), calls=%async_computation | async-start | bytes 2457600 | tf_op jit(solution)/shard_map/all_to_all | solution.py:134
  28.2 18.4 %copy-start = (bf16[24,12800]{1,0:T(8,128)(2,1)}, bf16[24,12800]{1,0:T(8,128)(2,1)S(1)}, u32[]{:S(2)}) copy-start(bf16[24,12800]{1,0:T(8,128)(2,1)S(1)} %get-tuple-element.18) | copy-start | bytes 1843204
  29.1 59.9 %collective-permute-start.11 = (bf16[4,12800]{1,0:T(4,128)(2,1)}, bf16[4,12800]{1,0:T(4,128)(2,1)}, u32[]{:S(2)}, u32[]{:S(2)}) collective-permute-start(bf16[4,12800]{1,0:T(4,128)(2,1)} %pad_maximum_fusion.11), channel_id=1, source_target_pairs={{0,64},{64,128},{128,192},{192,256},{256,320},{320,384},{384,448},... | collective-permute-start | bytes 307208 | tf_op jit(solution)/shard_map/ppermute | solution.py:27
  35.3 58.1 %collective-permute-start.10 = (bf16[4,12800]{1,0:T(4,128)(2,1)}, bf16[4,12800]{1,0:T(4,128)(2,1)}, u32[]{:S(2)}, u32[]{:S(2)}) collective-permute-start(bf16[4,12800]{1,0:T(4,128)(2,1)} %pad_maximum_fusion.10), channel_id=1, source_target_pairs={{0,128},{64,192},{128,256},{192,320},{256,384},{320,448},{384,512}... | collective-permute-start | bytes 307208 | tf_op jit(solution)/shard_map/ppermute | solution.py:27
  40.3 59.3 %collective-permute-start.9 = (bf16[4,12800]{1,0:T(4,128)(2,1)}, bf16[4,12800]{1,0:T(4,128)(2,1)}, u32[]{:S(2)}, u32[]{:S(2)}) collective-permute-start(bf16[4,12800]{1,0:T(4,128)(2,1)} %pad_maximum_fusion.9), channel_id=1, source_target_pairs={{0,192},{64,256},{128,320},{192,384},{256,448},{320,512},{384,576}... | collective-permute-start | bytes 307208 | tf_op jit(solution)/shard_map/ppermute | solution.py:27
  47.8 58.7 %collective-permute-start.8 = (bf16[4,12800]{1,0:T(4,128)(2,1)}, bf16[4,12800]{1,0:T(4,128)(2,1)}, u32[]{:S(2)}, u32[]{:S(2)}) collective-permute-start(bf16[4,12800]{1,0:T(4,128)(2,1)} %pad_maximum_fusion.8), channel_id=1, source_target_pairs={{0,256},{64,320},{128,384},{192,448},{256,512},{320,576},{384,640}... | collective-permute-start | bytes 307208 | tf_op jit(solution)/shard_map/ppermute | solution.py:27
  51.6 59.7 %collective-permute-start.7 = (bf16[4,12800]{1,0:T(4,128)(2,1)}, bf16[4,12800]{1,0:T(4,128)(2,1)}, u32[]{:S(2)}, u32[]{:S(2)}) collective-permute-start(bf16[4,12800]{1,0:T(4,128)(2,1)} %pad_maximum_fusion.7), channel_id=1, source_target_pairs={{0,320},{64,384},{128,448},{192,512},{256,576},{320,640},{384,704}... | collective-permute-start | bytes 307208 | tf_op jit(solution)/shard_map/ppermute | solution.py:27
  78.7 64.3 %all-to-all-start.1 = ((f32[32,1,1024]{2,1,0:T(1,128)}), f32[32,1,1024]{2,1,0:T(1,128)}, u32[]{:S(2)}, u32[]{:S(2)}) async-start(f32[32,1,1024]{2,1,0:T(1,128)} %bitcast.5), calls=%async_computation.1 | async-start | bytes 262144 | tf_op jit(solution)/shard_map/all_to_all | solution.py:31
  89.0 24.2 %collective-permute-start.6 = (bf16[4,12800]{1,0:T(4,128)(2,1)}, bf16[4,12800]{1,0:T(4,128)(2,1)S(1)}, u32[]{:S(2)}, u32[]{:S(2)}) collective-permute-start(bf16[4,12800]{1,0:T(4,128)(2,1)} %pad_maximum_fusion.6), channel_id=1, source_target_pairs={{0,384},{64,448},{128,512},{192,576},{256,640},{320,704},{384,0},{... | collective-permute-start | bytes 307208 | tf_op jit(solution)/shard_map/ppermute | solution.py:27
  93.4 25.0 %collective-permute-start.5 = (bf16[4,12800]{1,0:T(4,128)(2,1)}, bf16[4,12800]{1,0:T(4,128)(2,1)S(1)}, u32[]{:S(2)}, u32[]{:S(2)}) collective-permute-start(bf16[4,12800]{1,0:T(4,128)(2,1)} %pad_maximum_fusion.5), channel_id=1, source_target_pairs={{0,448},{64,512},{128,576},{192,640},{256,704},{320,0},{384,64},{4... | collective-permute-start | bytes 307208 | tf_op jit(solution)/shard_map/ppermute | solution.py:27
  99.7 22.1 %collective-permute-start.4 = (bf16[4,12800]{1,0:T(4,128)(2,1)}, bf16[4,12800]{1,0:T(4,128)(2,1)S(1)}, u32[]{:S(2)}, u32[]{:S(2)}) collective-permute-start(bf16[4,12800]{1,0:T(4,128)(2,1)} %pad_maximum_fusion.4), channel_id=1, source_target_pairs={{0,512},{64,576},{128,640},{192,704},{256,0},{320,64},{384,128},{4... | collective-permute-start | bytes 307208 | tf_op jit(solution)/shard_map/ppermute | solution.py:27
  106.5 22.1 %collective-permute-start.3 = (bf16[4,12800]{1,0:T(4,128)(2,1)}, bf16[4,12800]{1,0:T(4,128)(2,1)S(1)}, u32[]{:S(2)}, u32[]{:S(2)}) collective-permute-start(bf16[4,12800]{1,0:T(4,128)(2,1)} %pad_maximum_fusion.3), channel_id=1, source_target_pairs={{0,576},{64,640},{128,704},{192,0},{256,64},{320,128},{384,192},{4... | collective-permute-start | bytes 307208 | tf_op jit(solution)/shard_map/ppermute | solution.py:27
  111.3 22.0 %collective-permute-start.2 = (bf16[4,12800]{1,0:T(4,128)(2,1)}, bf16[4,12800]{1,0:T(4,128)(2,1)S(1)}, u32[]{:S(2)}, u32[]{:S(2)}) collective-permute-start(bf16[4,12800]{1,0:T(4,128)(2,1)} %pad_maximum_fusion.2), channel_id=1, source_target_pairs={{0,640},{64,704},{128,0},{192,64},{256,128},{320,192},{384,256},{4... | collective-permute-start | bytes 307208 | tf_op jit(solution)/shard_map/ppermute | solution.py:27
  113.2 20.1 %copy-start.2 = (bf16[4,12800]{1,0:T(4,128)(2,1)}, bf16[4,12800]{1,0:T(4,128)(2,1)S(1)}, u32[]{:S(2)}) copy-start(bf16[4,12800]{1,0:T(4,128)(2,1)S(1)} %collective-permute-done.6) | copy-start | bytes 307204
  113.2 22.0 %collective-permute-start.1 = (bf16[4,12800]{1,0:T(4,128)(2,1)S(1)}, bf16[4,12800]{1,0:T(4,128)(2,1)}, u32[]{:S(2)}, u32[]{:S(2)}) collective-permute-start(bf16[4,12800]{1,0:T(4,128)(2,1)S(1)} %pad_maximum_fusion.1), channel_id=1, source_target_pairs={{0,704},{64,0},{128,64},{192,128},{256,192},{320,256},{384,320},{4... | collective-permute-start | bytes 307208 | tf_op jit(solution)/shard_map/ppermute | solution.py:27
  118.4 15.0 %copy-start.3 = (bf16[4,12800]{1,0:T(4,128)(2,1)}, bf16[4,12800]{1,0:T(4,128)(2,1)S(1)}, u32[]{:S(2)}) copy-start(bf16[4,12800]{1,0:T(4,128)(2,1)S(1)} %collective-permute-done.5) | copy-start | bytes 307204
  121.8 11.6 %copy-start.4 = (bf16[4,12800]{1,0:T(4,128)(2,1)}, bf16[4,12800]{1,0:T(4,128)(2,1)S(1)}, u32[]{:S(2)}) copy-start(bf16[4,12800]{1,0:T(4,128)(2,1)S(1)} %collective-permute-done.4) | copy-start | bytes 307204
  128.6 4.7 %copy-start.5 = (bf16[4,12800]{1,0:T(4,128)(2,1)}, bf16[4,12800]{1,0:T(4,128)(2,1)S(1)}, u32[]{:S(2)}) copy-start(bf16[4,12800]{1,0:T(4,128)(2,1)S(1)} %collective-permute-done.3) | copy-start | bytes 307204
  133.3 0.6 copy-start.6
  144.7 16.8 %all-to-all-start.2 = ((f32[24,1,1024]{2,1,0:T(1,128)}), f32[24,1,1024]{2,1,0:T(1,128)S(1)}, u32[]{:S(2)}, u32[]{:S(2)}) async-start(f32[24,1,1024]{2,1,0:T(1,128)} %broadcast_in_dim.7), calls=%async_computation.2 | async-start | bytes 196608 | tf_op jit(solution)/shard_map/all_to_all | solution.py:31
  162.3 18.7 %all-to-all-start.3 = ((f32[32,1,1024]{2,1,0:T(1,128)}), f32[32,1,1024]{2,1,0:T(1,128)S(1)}, u32[]{:S(2)}, u32[]{:S(2)}) async-start(f32[32,1,1024]{2,1,0:T(1,128)} %broadcast_in_dim.8), calls=%async_computation.3 | async-start | bytes 262144 | tf_op jit(solution)/shard_map/all_to_all | solution.py:31
